TPU v7x, 32 devices: a 4x2x2 block of a 4x4x8 slice. The times are simulated.
32 devices in a mesh: data: 4 (over y, z), seq: 8 (over x, core).
Axes of the slice: x: 4, y: 2, z: 2, core: 2. Of those that a mesh axis runs over, the one named last changes fastest.
The devices are a block of a 4x4x8 slice.
Arguments:
- patches: bfloat16 [256, 1024, 256], P('data', 'seq'), parts along dimension 0
- ln1_gain: float32 [256], replicated
- ln1_bias: float32 [256], replicated
- w_in: bfloat16 [256, 1536], replicated
- b_in: float32 [1536], replicated
- ln2_gain: float32 [768], replicated
- ln2_bias: float32 [768], replicated
- w_spatial: bfloat16 [1024, 1024], replicated
- b_spatial: float32 [1024], replicated
- w_out: bfloat16 [768, 256], replicated
- b_out: float32 [256], replicated
Outputs:
- output: bfloat16 [256, 1024, 256], P('data', 'seq'), parts along dimension 0
There are 4 independent parts. A program takes and returns all parts, laid end to end along the dimension named above; an argument that names none is the same for every part.
All inputs are finite; a program needn't handle non-finite values.
Results may differ from a plain program's by a relative error of at most 0.00919827.
Values are sent between devices in bfloat16 or wider.
A program may use at most 768 MiB of HBM per device.

v0:
```python
import jax
import jax.numpy as jnp
from jax import lax
from jax.sharding import PartitionSpec as P, NamedSharding

LN_EPS = 1e-6


def layer_norm(values, gain_vec, offset):
    values_f = values.astype(jnp.float32)
    mean_val = jnp.mean(values_f, axis=-1, keepdims=True)
    centered = values_f - mean_val
    var_val = jnp.mean(centered * centered, axis=-1, keepdims=True)
    return (centered * lax.rsqrt(var_val + LN_EPS) * gain_vec + offset).astype(jnp.bfloat16)


def gelu_proj(normed, weight, offset):
    hidden = jnp.einsum("bsc,cf->bsf", normed, weight, preferred_element_type=jnp.float32) + offset
    return jax.nn.gelu(hidden, approximate=False).astype(jnp.bfloat16)


def solution(mesh):
    row_spec = P("data", "seq", None)
    vec_spec = P(None)
    mat_spec = P(None, None)
    in_specs = (row_spec, vec_spec, vec_spec, mat_spec, vec_spec, vec_spec, vec_spec, mat_spec, vec_spec, mat_spec, vec_spec)

    def per_device(patches, ln1_gain, ln1_bias, w_in, b_in, ln2_gain, ln2_bias, w_spatial, b_spatial, w_out, b_out):
        half_dim = w_out.shape[0]
        local_rows = patches.shape[1]
        normed = layer_norm(patches, ln1_gain, ln1_bias)
        gate_a = gelu_proj(normed, w_in[:, :half_dim], b_in[:half_dim])
        gate_n = layer_norm(gelu_proj(normed, w_in[:, half_dim:], b_in[half_dim:]), ln2_gain, ln2_bias)
        by_channel = lax.all_to_all(gate_n, "seq", 2, 1, tiled=True)
        spatial = jnp.einsum("rs,bre->bse", w_spatial, by_channel, preferred_element_type=jnp.float32).astype(jnp.bfloat16)
        by_patch = lax.all_to_all(spatial, "seq", 1, 2, tiled=True)
        local_bias = lax.dynamic_slice_in_dim(b_spatial, lax.axis_index("seq") * local_rows, local_rows)
        gated = (gate_a.astype(jnp.float32) * (by_patch.astype(jnp.float32) + local_bias[:, None])).astype(jnp.bfloat16)
        mixed = jnp.einsum("bse,ec->bsc", gated, w_out, preferred_element_type=jnp.float32) + b_out
        return (patches.astype(jnp.float32) + mixed).astype(jnp.bfloat16)

    return jax.shard_map(per_device, mesh=mesh, in_specs=in_specs, out_specs=row_spec, check_vma=False)
```

profile of v0, /device:TPU:81, one launch (start us, length us, event | category | flops | bytes accessed | tf_op | source)
XLA Modules:
  0.0 689.4 jit_solution(15854855837659024269)
XLA Ops:
  0.0 0.0 copy-start
  0.0 3.5 convert_reduce_fusion.1
  3.5 4.0 fusion.29
  7.5 1.4 fusion.77
  8.9 64.3 %convert_reduce_fusion = (f32[64,128]{1,0:T(8,128)S(1)}, bf16[64,128,768]{2,1,0:T(8,128)(2,1)}) fusion(f32[768]{0:T(1024)S(1)} %get-tuple-element.6, bf16[256,1536]{1,0:T(8,128)(2,1)} %param.14, bf16[64,128,256]{2,1,0:T(8,128)(2,1)} %param.11, f32[256]{0:T(256)} %param.13, f32[256]{0:T(256)} %param.12, f32[64,128]{1,0:T(8,128)S(1)} %add_rsqrt_fusion.1, ...), kind=kOutput, calls=%fused_computation.3 | convolution fusion | flops 3661619200 | bytes 17273856 | tf_op jit(solution)/shard_map/bsc,cf->bsf/dot_general | solution.py:18
  73.2 8.3 %fusion.2 = f32[64,128]{1,0:T(8,128)S(1)} fusion(bf16[64,128,768]{2,1,0:T(8,128)(2,1)} %get-tuple-element.8, f32[64,128]{1,0:T(8,128)S(1)} %broadcast_multiply_fusion), kind=kLoop, calls=%fused_computation.6 | loop fusion | flops 25157632 | bytes 12648448 | tf_op jit(solution)/shard_map/reduce_sum | solution.py:13
  81.5 0.0 copy-done.3
  81.5 0.0 copy-done.4
  81.5 12.6 %fusion.5 = bf16[64,128,768]{2,1,0:T(8,128)(2,1)} fusion(bf16[64,128,768]{2,1,0:T(8,128)(2,1)} %get-tuple-element.8, f32[768]{0:T(1024)S(1)} %copy-done.3, f32[768]{0:T(1024)S(1)} %copy-done.4, f32[64,128]{1,0:T(8,128)S(1)} %add_rsqrt_fusion, f32[64,128]{1,0:T(8,128)S(1)} %broadcast_multiply_fusion), kind=kLoop, calls=%fused_computation.9 | loop fusion | flops 37748736 | bytes 25237504 | tf_op jit(solution)/shard_map/convert_element_type | solution.py:14
  94.2 16.7 %copy.30 = bf16[64,128,768]{1,0,2:T(8,128)(2,1)} copy(bf16[64,128,768]{2,1,0:T(8,128)(2,1)} %fusion.5) | data formatting | bytes 25165824 | tf_op jit(solution)/shard_map/convert_element_type | solution.py:14
  110.9 144.6 %all_to_all.27 = bf16[64,128,768]{1,0,2:T(8,128)(2,1)S(1)} all-to-all(bf16[64,128,768]{1,0,2:T(8,128)(2,1)} %copy.30), channel_id=1, replica_groups=mesh['data'=4,'seq'=8] {'seq'}, dimensions={2} | all-to-all | bytes 25165824 | tf_op jit(solution)/shard_map/all_to_all | solution.py:34
  255.5 28.5 %copy.32 = bf16[64,8,128,96]{2,1,3,0:T(8,128)(2,1)} copy(bf16[64,8,128,96]{2,0,3,1:T(8,128)(2,1)S(1)} %bitcast.45) | data formatting | bytes 25165824 | tf_op jit(solution)/shard_map/all_to_all | solution.py:34
  284.0 19.3 %all_to_all.23 = bf16[64,1024,96]{1,2,0:T(8,128)(2,1)} reshape(bf16[64,8,128,96]{2,1,3,0:T(8,128)(2,1)} %copy.32) | data formatting | bytes 25165824 | tf_op jit(solution)/shard_map/all_to_all | solution.py:34
  303.3 0.0 copy-done
  303.3 20.2 %convert_bitcast_fusion = bf16[64,1024,96]{1,2,0:T(8,128)(2,1)} fusion(bf16[64,1024,96]{1,2,0:T(8,128)(2,1)} %all_to_all.23, bf16[1024,1024]{1,0:T(8,128)(2,1)S(1)} %copy-done), kind=kOutput, calls=%fused_computation.47 | convolution fusion | flops 12891193344 | bytes 27262976 | tf_op jit(solution)/shard_map/rs,bre->bse/dot_general | solution.py:35
  323.5 21.8 %copy.33 = bf16[64,1024,96]{2,0,1:T(8,128)(2,1)} copy(bf16[64,1024,96]{1,2,0:T(8,128)(2,1)} %convert_bitcast_fusion) | data formatting | bytes 25165824 | tf_op jit(solution)/shard_map/convert_element_type | solution.py:35
  345.3 6.7 all-to-all-start.1
  352.0 0.8 dynamic_slice.3
  352.8 182.7 %all-to-all-done.1 = bf16[64,1024,96]{2,0,1:T(8,128)(2,1)} async-done(((bf16[64,1024,96]{2,0,1:T(8,128)(2,1)}), bf16[64,1024,96]{2,0,1:T(8,128)(2,1)}, u32[]{:S(2)}, u32[]{:S(2)}) %all-to-all-start.1) | async-done | bytes 12582944 | tf_op jit(solution)/shard_map/all_to_all | solution.py:36
  535.5 22.5 %copy.34 = bf16[64,1024,96]{1,2,0:T(8,128)(2,1)} copy(bf16[64,1024,96]{2,0,1:T(8,128)(2,1)} %all-to-all-done.1) | data formatting | bytes 25165824 | tf_op jit(solution)/shard_map/all_to_all | solution.py:36
  558.0 7.2 %convert_element_type.63 = f32[64,1024,96]{1,2,0:T(8,128)S(1)} convert(bf16[64,1024,96]{1,2,0:T(8,128)(2,1)} %copy.34) | non-fusion elementwise | flops 6291456 | bytes 37748736 | tf_op jit(solution)/shard_map/convert_element_type | solution.py:38
  565.1 11.2 %copy.38 = f32[768,8,8,128]{3,2,1,0:T(8,128)} copy(f32[768,8,8,128]{3,1,2,0:T(8,128)S(1)} %bitcast.42) | data formatting | bytes 50331648
  576.3 21.0 %copy.35 = f32[64,128,8,96]{1,3,2,0:T(8,128)} copy(f32[64,128,8,96]{1,2,3,0:T(8,128)} %bitcast.43) | data formatting | bytes 50331648 | tf_op jit(solution)/shard_map/convert_element_type | solution.py:38
  597.4 24.7 %copy.36 = f32[64,128,768]{2,1,0:T(8,128)} copy(f32[64,128,768]{1,2,0:T(8,128)} %bitcast.44) | data formatting | bytes 50331648 | tf_op jit(solution)/shard_map/convert_element_type | solution.py:38
  622.1 0.0 copy-done.5
  622.1 0.0 copy-done.8
  622.1 0.0 copy-start.2
  622.1 0.0 copy-start.7
  622.1 0.0 copy-start.10
  622.1 0.0 copy-start.1
  622.2 62.1 %multiply_convert_fusion.6 = bf16[64,128,768]{2,1,0:T(8,128)(2,1)S(1)} fusion(f32[64,128,768]{2,1,0:T(8,128)} %copy.36, f32[128]{0:T(128)S(1)} %dynamic_slice.3, f32[768]{0:T(1024)S(1)} %copy-done.5, bf16[64,128,256]{2,1,0:T(8,128)(2,1)} %param.11, f32[256]{0:T(256)S(1)} %copy-done.8, f32[256]{0:T(256)S(1)} %copy-done.9, ...), kind=kOutput, calls=%fused_computation.16.clone.clone.clone.clone.1 | convolution fusion | flops 3674210304 | bytes 42408448 | tf_op jit(solution)/shard_map/bsc,cf->bsf/dot_general | solution.py:18
  684.3 5.1 fusion.33
  (16 shorter events, 0.1 us)
Async XLA Ops:
  0.0 303.3 %copy-start = (bf16[1024,1024]{1,0:T(8,128)(2,1)S(1)}, bf16[1024,1024]{1,0:T(8,128)(2,1)}, u32[]{:S(2)}) copy-start(bf16[1024,1024]{1,0:T(8,128)(2,1)} %param.18) | copy-start | bytes 6291460
  8.9 72.6 %copy-start.3 = (f32[768]{0:T(1024)S(1)}, f32[768]{0:T(1024)}, u32[]{:S(2)}) copy-start(f32[768]{0:T(1024)} %param.17) | copy-start | bytes 9220
  8.9 72.6 %copy-start.4 = (f32[768]{0:T(1024)S(1)}, f32[768]{0:T(1024)}, u32[]{:S(2)}) copy-start(f32[768]{0:T(1024)} %param.16) | copy-start | bytes 9220
  345.3 190.2 %all-to-all-start.1 = ((bf16[64,1024,96]{2,0,1:T(8,128)(2,1)}), bf16[64,1024,96]{2,0,1:T(8,128)(2,1)}, u32[]{:S(2)}, u32[]{:S(2)}) async-start(bf16[64,1024,96]{2,0,1:T(8,128)(2,1)} %copy.33), calls=%async_computation.1 | async-start | bytes 33554432 | tf_op jit(solution)/shard_map/all_to_all | solution.py:36
  597.3 24.7 %copy-start.5 = (f32[768]{0:T(1024)S(1)}, f32[768]{0:T(1024)}, u32[]{:S(2)}) copy-start(f32[768]{0:T(1024)} %get-tuple-element.5) | copy-start | bytes 9220
  597.3 24.7 %copy-start.6 = (bf16[256,1536]{1,0:T(8,128)(2,1)S(1)}, bf16[256,1536]{1,0:T(8,128)(2,1)}, u32[]{:S(2)}) copy-start(bf16[256,1536]{1,0:T(8,128)(2,1)} %param.14) | copy-start | bytes 2359300
  597.3 24.7 %copy-start.8 = (f32[256]{0:T(256)S(1)}, f32[256]{0:T(256)}, u32[]{:S(2)}) copy-start(f32[256]{0:T(256)} %param.13) | copy-start | bytes 3076
  597.3 24.8 %copy-start.9 = (f32[256]{0:T(256)S(1)}, f32[256]{0:T(256)}, u32[]{:S(2)}) copy-start(f32[256]{0:T(256)} %param.12) | copy-start | bytes 3076
  622.1 62.2 %copy-start.2 = (bf16[64,128,256]{2,1,0:T(8,128)(2,1)S(1)}, bf16[64,128,256]{2,1,0:T(8,128)(2,1)}, u32[]{:S(2)}) copy-start(bf16[64,128,256]{2,1,0:T(8,128)(2,1)} %param.11) | copy-start | bytes 12582916
  622.1 62.2 %copy-start.7 = (bf16[768,256]{1,0:T(8,128)(2,1)S(1)}, bf16[768,256]{1,0:T(8,128)(2,1)}, u32[]{:S(2)}) copy-start(bf16[768,256]{1,0:T(8,128)(2,1)} %param.20) | copy-start | bytes 1179652
  622.1 62.2 %copy-start.10 = (f32[256]{0:T(256)S(1)}, f32[256]{0:T(256)}, u32[]{:S(2)}) copy-start(f32[256]{0:T(256)} %param.21) | copy-start | bytes 3076
  622.1 67.3 %copy-start.1 = (bf16[1024,1024]{1,0:T(8,128)(2,1)S(1)}, bf16[1024,1024]{1,0:T(8,128)(2,1)}, u32[]{:S(2)}) copy-start(bf16[1024,1024]{1,0:T(8,128)(2,1)} %param.18) | copy-start | bytes 6291460
where the time goes:
time: 692 us; the launch traced here: 689 us
  waiting for transfers between devices  183 us (26%)
  local copies, waits for them, and re-layouts  168 us (24%)
  matrix products  152 us (22%)
  blocking collectives  145 us (21%)
  other arithmetic  35.6 us (5%)
    all_to_all x1, waiting for transfers between devices, per_device(): by_patch = lax.all_to_all(spatial, 'seq', 1, 2, tiled=True)  183 us
    all_to_all x1, blocking collectives, per_device(): by_channel = lax.all_to_all(gate_n, 'seq', 2, 1, tiled=True)  145 us
    dot_general x2, matrix products, gelu_proj(): jnp.einsum('bsc,cf->bsf', normed, weight, preferred_element_type=jnp.floa...  126 us
    all_to_all x2, local copies, waits for them, and re-layouts, per_device(): by_channel = lax.all_to_all(gate_n, 'seq', 2, 1, tiled=True)  47.8 us
    convert_element_type x2, local copies, waits for them, and re-layouts, per_device(): by_patch.astype(jnp.float32) + local_bias[:, None]  45.7 us
    all_to_all x1, local copies, waits for them, and re-layouts, per_device(): by_patch = lax.all_to_all(spatial, 'seq', 1, 2, tiled=True)  22.5 us
    convert_element_type x1, local copies, waits for them, and re-layouts, per_device(): jnp.einsum('rs,bre->bse', w_spatial, by_channel, preferred_element_type=j...  21.8 us
    dot_general x1, matrix products, per_device(): jnp.einsum('rs,bre->bse', w_spatial, by_channel, preferred_element_type=j...  20.2 us
  transfers between devices with their start and end apart: 1, of which 1 were waited for; matrix products, arithmetic and copies ran while one was open for 0% of the time, Pallas kernels for 0%

commit v1 on v0

v1 whole, which is shorter than its diff:
```python
import functools

import jax
import jax.numpy as jnp
from jax import lax
from jax.experimental import pallas as pl
from jax.experimental.pallas import tpu as pltpu
from jax.sharding import PartitionSpec as P

LN_EPS = 1e-6
MESH = pl.DeviceIdType.MESH
F32 = jnp.float32
BF16 = jnp.bfloat16
TILE = 256


def layer_norm(values, gain_vec, offset):
    values_f = values.astype(F32)
    mean_val = jnp.mean(values_f, axis=-1, keepdims=True)
    centered = values_f - mean_val
    var_val = jnp.mean(centered * centered, axis=-1, keepdims=True)
    return (centered * lax.rsqrt(var_val + LN_EPS) * gain_vec + offset).astype(BF16)


def gelu(hidden):
    half = 0.5 * hidden
    return (half + half * lax.erf(hidden * (0.5 ** 0.5))).astype(BF16)


def block_kernel(n_seq, axis, x_hbm, ln1_gain, ln1_bias, w_in_hbm, b_in, ln2_gain, ln2_bias, w_spatial_hbm, b_spatial, w_out_hbm,
                 b_out, out_hbm, x_buf, o_buf, n_buf, a_buf, w_in, w_out, w_spatial, w_mix, bias_col, in_send, in_recv,
                 out_send, out_recv, w_sem):
    me = lax.axis_index(axis)
    images, rows, _ = x_hbm.shape
    own = images // n_seq
    patches = rows * n_seq
    half_dim = w_out.shape[0]
    per_tile = TILE // rows
    tiles = patches // TILE
    home = me // per_tile

    barrier = pltpu.get_barrier_semaphore()
    for off in range(1, n_seq):
        pl.semaphore_signal(barrier, inc=1, device_id={axis: lax.rem(me + off, n_seq)}, device_id_type=MESH)
    pl.semaphore_wait(barrier, n_seq - 1)

    def block_rows(dev):
        return pl.ds(pl.multiple_of(dev * rows, rows), rows)

    @pl.loop(0, own)
    def _(slot):
        for off in range(1, n_seq):
            dev = lax.rem(me + off, n_seq)
            pltpu.make_async_remote_copy(
                src_ref=x_hbm.at[dev * own + slot],
                dst_ref=x_buf.at[slot, block_rows(me)],
                send_sem=in_send.at[off],
                recv_sem=in_recv.at[slot],
                device_id={axis: dev},
                device_id_type=MESH,
            ).start()
        pltpu.make_async_copy(x_hbm.at[me * own + slot], x_buf.at[slot, block_rows(me)], in_recv.at[slot]).start()

    weights = [
        pltpu.make_async_copy(w_spatial_hbm, w_spatial, w_sem.at[0]),
        pltpu.make_async_copy(w_in_hbm, w_in, w_sem.at[1]),
        pltpu.make_async_copy(w_out_hbm, w_out, w_sem.at[2]),
    ]
    for copy in weights:
        copy.start()
    for first in range(0, patches, 128):
        lane_bias = jnp.broadcast_to(b_spatial[:, first:first + 128], (128, 128))
        bias_col[first:first + 128, :] = lane_bias.T
    weights[0].wait()

    @pl.loop(0, patches // TILE)
    def _(step):
        out_rows = pl.ds(pl.multiple_of(step * TILE, TILE), TILE)
        for first in range(0, patches, TILE):
            w_mix[out_rows, first:first + TILE] = w_spatial[first:first + TILE, out_rows].T

    weights[1].wait()
    weights[2].wait()

    def send_tile(slot, tile):
        for part in range(per_tile):
            dev = tile * per_tile + part
            pltpu.make_async_remote_copy(
                src_ref=o_buf.at[slot, block_rows(dev)],
                dst_ref=out_hbm.at[me * own + slot],
                send_sem=out_send.at[0],
                recv_sem=out_recv.at[me],
                device_id={axis: dev},
                device_id_type=MESH,
            ).start()

    def send_home(slot):
        pltpu.make_async_copy(o_buf.at[slot, block_rows(me)], out_hbm.at[me * own + slot], out_recv.at[me]).start()
        for step in range(1, per_tile):
            dev = home * per_tile + lax.rem(me + step, per_tile)
            pltpu.make_async_remote_copy(
                src_ref=o_buf.at[slot, block_rows(dev)],
                dst_ref=out_hbm.at[me * own + slot],
                send_sem=out_send.at[0],
                recv_sem=out_recv.at[me],
                device_id={axis: dev},
                device_id_type=MESH,
            ).start()

    @pl.loop(0, own)
    def _(slot):
        pltpu.make_async_copy(x_buf.at[slot], x_buf.at[slot], in_recv.at[slot]).wait()

        @pl.loop(0, tiles)
        def _(tile):
            here = pl.ds(pl.multiple_of(tile * TILE, TILE), TILE)
            normed = layer_norm(x_buf[slot, here, :], ln1_gain[...], ln1_bias[...])
            gate = []
            for first in range(0, 2 * half_dim, 256):
                cols = slice(first, first + 256)
                hidden = jnp.dot(normed, w_in[:, cols], preferred_element_type=F32) + b_in[:, cols]
                act = gelu(hidden)
                if first < half_dim:
                    a_buf[here, cols] = act
                else:
                    gate.append(act)
            gate = jnp.concatenate(gate, axis=1)
            n_buf[here, :] = layer_norm(gate, ln2_gain[...], ln2_bias[...])

        @pl.when(slot > 0)
        def _():
            send_home(slot - 1)

        @pl.loop(0, tiles)
        def _(step):
            tile = lax.rem(home + 1 + step, tiles)
            here = pl.ds(pl.multiple_of(tile * TILE, TILE), TILE)
            spatial = jnp.dot(w_mix[here, :], n_buf[...], preferred_element_type=F32).astype(BF16)
            bias = jnp.tile(bias_col[here, :], (1, half_dim // 128))
            gated = (a_buf[here, :].astype(F32) * (spatial.astype(F32) + bias)).astype(BF16)
            mixed = jnp.dot(gated, w_out[...], preferred_element_type=F32) + b_out[...]
            o_buf[slot, here, :] = (x_buf[slot, here, :].astype(F32) + mixed).astype(BF16)

            @pl.when(step > 0)
            def _():
                send_tile(slot, lax.rem(home + step, tiles))

    send_home(own - 1)

    for off in range(1, n_seq):
        dev = lax.rem(me + off, n_seq)
        pltpu.make_async_copy(x_hbm.at[pl.ds(0, own)], x_hbm.at[pl.ds(0, own)], in_send.at[off]).wait()
    sent = o_buf.at[:, pl.ds(0, rows * (n_seq - 1))]
    pltpu.make_async_copy(sent, sent, out_send.at[0]).wait()
    for dev in range(n_seq):
        part = out_hbm.at[pl.ds(dev * own, own)]
        pltpu.make_async_copy(part, part, out_recv.at[dev]).wait()


def solution(mesh):
    row_spec = P("data", "seq", None)
    vec_spec = P(None)
    mat_spec = P(None, None)
    in_specs = (row_spec, vec_spec, vec_spec, mat_spec, vec_spec, vec_spec, vec_spec, mat_spec, vec_spec, mat_spec, vec_spec)
    n_seq = mesh.shape["seq"]

    def per_device(patches, ln1_gain, ln1_bias, w_in, b_in, ln2_gain, ln2_bias, w_spatial, b_spatial, w_out, b_out):
        images, rows, dim = patches.shape
        own = images // n_seq
        total = rows * n_seq
        half_dim = w_out.shape[0]
        hbm = pl.BlockSpec(memory_space=pl.ANY)
        vmem = pl.BlockSpec(memory_space=pltpu.VMEM)
        row = lambda vec: vec.reshape(1, vec.shape[0])
        return pl.pallas_call(
            functools.partial(block_kernel, n_seq, "seq"),
            out_shape=jax.ShapeDtypeStruct(patches.shape, BF16),
            in_specs=[hbm, vmem, vmem, hbm, vmem, vmem, vmem, hbm, vmem, hbm, vmem],
            out_specs=hbm,
            scratch_shapes=[
                pltpu.VMEM((own, total, dim), BF16),
                pltpu.VMEM((own, total, dim), BF16),
                pltpu.VMEM((total, half_dim), BF16),
                pltpu.VMEM((total, half_dim), BF16),
                pltpu.VMEM(w_in.shape, BF16),
                pltpu.VMEM(w_out.shape, BF16),
                pltpu.VMEM(w_spatial.shape, BF16),
                pltpu.VMEM(w_spatial.shape, BF16),
                pltpu.VMEM((total, 128), F32),
                pltpu.SemaphoreType.DMA((n_seq,)),
                pltpu.SemaphoreType.DMA((own,)),
                pltpu.SemaphoreType.DMA((1,)),
                pltpu.SemaphoreType.DMA((n_seq,)),
                pltpu.SemaphoreType.DMA((3,)),
            ],
            compiler_params=pltpu.CompilerParams(
                collective_id=0, has_side_effects=True, vmem_limit_bytes=48 * 1024 * 1024
            ),
            name="gmlp_block",
        )(patches, row(ln1_gain), row(ln1_bias), w_in, row(b_in), row(ln2_gain), row(ln2_bias), w_spatial, row(b_spatial),
          w_out, row(b_out))

    return jax.shard_map(per_device, mesh=mesh, in_specs=in_specs, out_specs=row_spec, check_vma=False)
```

time: 692 us -> 110 us (0.16)
  waiting for transfers between devices: 183 us -> 0 us
  local copies, waits for them, and re-layouts: 168 us -> 13.2 us
  matrix products: 152 us -> 0 us
  blocking collectives: 145 us -> 0 us
  Pallas kernels: 0 us -> 96.8 us
  other arithmetic: 35.6 us -> 0 us
    all_to_all x1 -> x0, waiting for transfers between devices: 183 us -> none  [per_device(): by_patch = lax.all_to_all(spatial, 'seq', 1, 2, tiled=True)]
    dot_general x4 -> x0, matrix products: 152 us -> none  [the longest x2 126 us: gelu_proj(): jnp.einsum('bsc,cf->bsf', normed, weight, preferred_element_type=jnp.floa...]
    all_to_all x1 -> x0, blocking collectives: 145 us -> none  [per_device(): by_channel = lax.all_to_all(gate_n, 'seq', 2, 1, tiled=True)]
    pallas_call x0 -> x1, Pallas kernels: none -> 96.8 us  [per_device(): pl.pallas_call(functools.partial(block_kernel, n_seq, 'seq'), out_shape=j...]
    convert_element_type x4 -> x0, local copies, waits for them, and re-layouts: 84.2 us -> none  [the longest x2 45.7 us: per_device(): by_patch.astype(jnp.float32) + local_bias[:, None]]
    all_to_all x3 -> x0, local copies, waits for them, and re-layouts: 70.2 us -> none  [the longest x2 47.8 us: per_device(): by_channel = lax.all_to_all(gate_n, 'seq', 2, 1, tiled=True)]
    convert_element_type x2 -> x0, other arithmetic: 19.8 us -> none  [the longest x1 12.6 us: layer_norm(): (centered * lax.rsqrt(var_val + LN_EPS) * gain_vec + offset).astype(jnp.b...]
    reduce_sum x3 -> x0, other arithmetic: 15.8 us -> none  [the longest x2 12.3 us: layer_norm(): var_val = jnp.mean(centered * centered, axis=-1, keepdims=True)]
  transfers between devices with their start and end apart: 1 -> 0, of which waited for: 1 -> 0; matrix products, arithmetic and copies ran while one was open for 0% -> 0% of each run, Pallas kernels for 0% -> 0%
where the time goes in v1:
time: 110 us
  Pallas kernels  96.8 us (88%)
  local copies, waits for them, and re-layouts  13.2 us (12%)
    pallas_call x1, Pallas kernels, per_device(): pl.pallas_call(functools.partial(block_kernel, n_seq, 'seq'), out_shape=j...  96.8 us
    unnamed x15, local copies, waits for them, and re-layouts  11.1 us

profile of v1, /device:TPU:81, one launch (start us, length us, event | category | flops | bytes accessed | tf_op | source)
XLA Modules:
  0.0 110.0 jit_solution(3553058844852429847)
XLA Ops:
  0.0 0.7 reshape.24.ln2_gain
  0.7 0.7 reshape.25.ln2_bias
  1.4 0.7 reshape.23.b_in
  2.1 0.0 copy-start
  2.1 1.6 %copy-done = bf16[1024,1024]{1,0:T(8,128)(2,1)S(1)} copy-done((bf16[1024,1024]{1,0:T(8,128)(2,1)S(1)}, bf16[1024,1024]{1,0:T(8,128)(2,1)}, u32[]{:S(2)}) %copy-start) | copy-done | bytes 2097176
  3.7 0.0 copy-start.1
  3.7 1.1 %copy-done.1 = bf16[256,1536]{1,0:T(8,128)(2,1)S(1)} copy-done((bf16[256,1536]{1,0:T(8,128)(2,1)S(1)}, bf16[256,1536]{1,0:T(8,128)(2,1)}, u32[]{:S(2)}) %copy-start.1) | copy-done | bytes 786456
  4.8 0.0 copy-start.2
  4.8 1.0 copy-done.2
  5.8 0.0 copy-start.3
  5.8 0.7 copy-done.3
  6.5 0.0 copy-start.4
  6.5 0.7 copy-done.4
  7.2 0.0 copy-start.5
  7.2 0.7 copy-done.5
  7.8 0.0 copy-start.6
  7.9 0.7 copy-done.6
  8.5 96.8 %gmlp_block.1 = bf16[64,128,256]{2,1,0:T(8,128)(2,1)} custom-call(bf16[64,128,256]{2,1,0:T(8,128)(2,1)} %x_hbm.1, f32[1,256]{1,0:T(1,128)S(1)} %bitcast.5, f32[1,256]{1,0:T(1,128)S(1)} %bitcast.6, bf16[256,1536]{1,0:T(8,128)(2,1)S(1)} %copy-done.1, f32[1,1536]{1,0:T(1,128)S(1)} %reshape.23.b_in, f32[1,768]{1,0:T(1,128)S(1)} %reshape.24.ln2_gain, ...), custom_call_target="tpu_custom_call" | custom-call | tf_op jit(solution)/shard_map/gmlp_block/pallas_call | solution.py:175
  105.3 4.7 %copy.13 = bf16[64,128,256]{2,1,0:T(8,128)(2,1)} copy(bf16[64,128,256]{2,1,0:T(8,128)(2,1)} %gmlp_block.1) | data formatting | bytes 8388608
Async XLA Ops:
  2.1 1.6 %copy-start = (bf16[1024,1024]{1,0:T(8,128)(2,1)S(1)}, bf16[1024,1024]{1,0:T(8,128)(2,1)}, u32[]{:S(2)}) copy-start(bf16[1024,1024]{1,0:T(8,128)(2,1)} %w_spatial_hbm.1) | copy-start | bytes 6291460
  3.7 1.1 %copy-start.1 = (bf16[256,1536]{1,0:T(8,128)(2,1)S(1)}, bf16[256,1536]{1,0:T(8,128)(2,1)}, u32[]{:S(2)}) copy-start(bf16[256,1536]{1,0:T(8,128)(2,1)} %w_in_hbm.1) | copy-start | bytes 2359300
  4.8 1.0 copy-start.2
  5.8 0.7 copy-start.3
  6.5 0.7 copy-start.4
  7.2 0.7 copy-start.5
  7.8 0.7 copy-start.6

commit v2 on v1

--- a/solution.py
+++ b/solution.py
@@ -22,14 +22,18 @@
     return (centered * lax.rsqrt(var_val + LN_EPS) * gain_vec + offset).astype(BF16)
 
 
+def as_row(ref):
+    return ref[...].reshape(1, ref.shape[0])
+
+
 def gelu(hidden):
     half = 0.5 * hidden
     return (half + half * lax.erf(hidden * (0.5 ** 0.5))).astype(BF16)
 
 
-def block_kernel(n_seq, axis, x_hbm, ln1_gain, ln1_bias, w_in_hbm, b_in, ln2_gain, ln2_bias, w_spatial_hbm, b_spatial, w_out_hbm,
-                 b_out, out_hbm, x_buf, o_buf, n_buf, a_buf, w_in, w_out, w_spatial, w_mix, bias_col, in_send, in_recv,
-                 out_send, out_recv, w_sem):
+def block_kernel(n_seq, axis, x_hbm, ln1_gain_hbm, ln1_bias_hbm, w_in_hbm, b_in_hbm, ln2_gain_hbm, ln2_bias_hbm, w_spatial_hbm,
+                 b_spatial_hbm, w_out_hbm, b_out_hbm, out_ref, x_buf, o_buf, n_buf, a_buf, ln1_gain, ln1_bias, w_in, b_in, ln2_gain,
+                 ln2_bias, w_spatial, b_spatial, w_out, b_out, w_mix, bias_col, in_send, in_recv, out_send, out_recv, w_sem):
     me = lax.axis_index(axis)
     images, rows, _ = x_hbm.shape
     own = images // n_seq
@@ -61,17 +65,18 @@
             ).start()
         pltpu.make_async_copy(x_hbm.at[me * own + slot], x_buf.at[slot, block_rows(me)], in_recv.at[slot]).start()
 
-    weights = [
-        pltpu.make_async_copy(w_spatial_hbm, w_spatial, w_sem.at[0]),
-        pltpu.make_async_copy(w_in_hbm, w_in, w_sem.at[1]),
-        pltpu.make_async_copy(w_out_hbm, w_out, w_sem.at[2]),
+    operands = [
+        (b_spatial_hbm, b_spatial), (w_spatial_hbm, w_spatial), (ln1_gain_hbm, ln1_gain), (ln1_bias_hbm, ln1_bias), (w_in_hbm, w_in),
+        (b_in_hbm, b_in), (ln2_gain_hbm, ln2_gain), (ln2_bias_hbm, ln2_bias), (w_out_hbm, w_out), (b_out_hbm, b_out),
     ]
-    for copy in weights:
-        copy.start()
+    loads = [pltpu.make_async_copy(src, dst, w_sem.at[k]) for k, (src, dst) in enumerate(operands)]
+    for load in loads:
+        load.start()
+    loads[0].wait()
     for first in range(0, patches, 128):
-        lane_bias = jnp.broadcast_to(b_spatial[:, first:first + 128], (128, 128))
+        lane_bias = jnp.broadcast_to(b_spatial[first:first + 128].reshape(1, 128), (128, 128))
         bias_col[first:first + 128, :] = lane_bias.T
-    weights[0].wait()
+    loads[1].wait()
 
     @pl.loop(0, patches // TILE)
     def _(step):
@@ -79,15 +84,15 @@
         for first in range(0, patches, TILE):
             w_mix[out_rows, first:first + TILE] = w_spatial[first:first + TILE, out_rows].T
 
-    weights[1].wait()
-    weights[2].wait()
+    for load in loads[2:]:
+        load.wait()
 
     def send_tile(slot, tile):
         for part in range(per_tile):
             dev = tile * per_tile + part
             pltpu.make_async_remote_copy(
                 src_ref=o_buf.at[slot, block_rows(dev)],
-                dst_ref=out_hbm.at[me * own + slot],
+                dst_ref=out_ref.at[me * own + slot],
                 send_sem=out_send.at[0],
                 recv_sem=out_recv.at[me],
                 device_id={axis: dev},
@@ -95,12 +100,12 @@
             ).start()
 
     def send_home(slot):
-        pltpu.make_async_copy(o_buf.at[slot, block_rows(me)], out_hbm.at[me * own + slot], out_recv.at[me]).start()
+        pltpu.make_async_copy(o_buf.at[slot, block_rows(me)], out_ref.at[me * own + slot], out_recv.at[me]).start()
         for step in range(1, per_tile):
             dev = home * per_tile + lax.rem(me + step, per_tile)
             pltpu.make_async_remote_copy(
                 src_ref=o_buf.at[slot, block_rows(dev)],
-                dst_ref=out_hbm.at[me * own + slot],
+                dst_ref=out_ref.at[me * own + slot],
                 send_sem=out_send.at[0],
                 recv_sem=out_recv.at[me],
                 device_id={axis: dev},
@@ -114,18 +119,18 @@
         @pl.loop(0, tiles)
         def _(tile):
             here = pl.ds(pl.multiple_of(tile * TILE, TILE), TILE)
-            normed = layer_norm(x_buf[slot, here, :], ln1_gain[...], ln1_bias[...])
+            normed = layer_norm(x_buf[slot, here, :], as_row(ln1_gain), as_row(ln1_bias))
             gate = []
             for first in range(0, 2 * half_dim, 256):
                 cols = slice(first, first + 256)
-                hidden = jnp.dot(normed, w_in[:, cols], preferred_element_type=F32) + b_in[:, cols]
+                hidden = jnp.dot(normed, w_in[:, cols], preferred_element_type=F32) + b_in[cols].reshape(1, 256)
                 act = gelu(hidden)
                 if first < half_dim:
                     a_buf[here, cols] = act
                 else:
                     gate.append(act)
             gate = jnp.concatenate(gate, axis=1)
-            n_buf[here, :] = layer_norm(gate, ln2_gain[...], ln2_bias[...])
+            n_buf[here, :] = layer_norm(gate, as_row(ln2_gain), as_row(ln2_bias))
 
         @pl.when(slot > 0)
         def _():
@@ -138,7 +143,7 @@
             spatial = jnp.dot(w_mix[here, :], n_buf[...], preferred_element_type=F32).astype(BF16)
             bias = jnp.tile(bias_col[here, :], (1, half_dim // 128))
             gated = (a_buf[here, :].astype(F32) * (spatial.astype(F32) + bias)).astype(BF16)
-            mixed = jnp.dot(gated, w_out[...], preferred_element_type=F32) + b_out[...]
+            mixed = jnp.dot(gated, w_out[...], preferred_element_type=F32) + as_row(b_out)
             o_buf[slot, here, :] = (x_buf[slot, here, :].astype(F32) + mixed).astype(BF16)
 
             @pl.when(step > 0)
@@ -153,7 +158,7 @@
     sent = o_buf.at[:, pl.ds(0, rows * (n_seq - 1))]
     pltpu.make_async_copy(sent, sent, out_send.at[0]).wait()
     for dev in range(n_seq):
-        part = out_hbm.at[pl.ds(dev * own, own)]
+        part = out_ref.at[pl.ds(dev * own, own)]
         pltpu.make_async_copy(part, part, out_recv.at[dev]).wait()
 
 
@@ -165,39 +170,36 @@
     n_seq = mesh.shape["seq"]
 
     def per_device(patches, ln1_gain, ln1_bias, w_in, b_in, ln2_gain, ln2_bias, w_spatial, b_spatial, w_out, b_out):
+        operands = (patches, ln1_gain, ln1_bias, w_in, b_in, ln2_gain, ln2_bias, w_spatial, b_spatial, w_out, b_out)
         images, rows, dim = patches.shape
         own = images // n_seq
         total = rows * n_seq
         half_dim = w_out.shape[0]
-        hbm = pl.BlockSpec(memory_space=pl.ANY)
-        vmem = pl.BlockSpec(memory_space=pltpu.VMEM)
-        row = lambda vec: vec.reshape(1, vec.shape[0])
+        hbm = pl.BlockSpec(memory_space=pltpu.HBM)
+        vec = lambda ref: pltpu.VMEM(ref.shape, ref.dtype)
         return pl.pallas_call(
             functools.partial(block_kernel, n_seq, "seq"),
-            out_shape=jax.ShapeDtypeStruct(patches.shape, BF16),
-            in_specs=[hbm, vmem, vmem, hbm, vmem, vmem, vmem, hbm, vmem, hbm, vmem],
-            out_specs=hbm,
+            out_shape=pltpu.VMEM(patches.shape, BF16),
+            in_specs=[hbm] * 11,
+            out_specs=pl.BlockSpec(memory_space=pltpu.VMEM),
             scratch_shapes=[
                 pltpu.VMEM((own, total, dim), BF16),
                 pltpu.VMEM((own, total, dim), BF16),
                 pltpu.VMEM((total, half_dim), BF16),
                 pltpu.VMEM((total, half_dim), BF16),
-                pltpu.VMEM(w_in.shape, BF16),
-                pltpu.VMEM(w_out.shape, BF16),
-                pltpu.VMEM(w_spatial.shape, BF16),
+                *[vec(v) for v in operands[1:]],
                 pltpu.VMEM(w_spatial.shape, BF16),
                 pltpu.VMEM((total, 128), F32),
                 pltpu.SemaphoreType.DMA((n_seq,)),
                 pltpu.SemaphoreType.DMA((own,)),
                 pltpu.SemaphoreType.DMA((1,)),
                 pltpu.SemaphoreType.DMA((n_seq,)),
-                pltpu.SemaphoreType.DMA((3,)),
+                pltpu.SemaphoreType.DMA((10,)),
             ],
             compiler_params=pltpu.CompilerParams(
                 collective_id=0, has_side_effects=True, vmem_limit_bytes=48 * 1024 * 1024
             ),
             name="gmlp_block",
-        )(patches, row(ln1_gain), row(ln1_bias), w_in, row(b_in), row(ln2_gain), row(ln2_bias), w_spatial, row(b_spatial),
-          w_out, row(b_out))
+        )(*[pltpu.with_memory_space_constraint(v, pltpu.HBM) for v in operands])
 
     return jax.shard_map(per_device, mesh=mesh, in_specs=in_specs, out_specs=row_spec, check_vma=False)

time: 110 us -> 98.9 us (0.90)
  local copies, waits for them, and re-layouts: 13.2 us -> 2.02 us
    unnamed x15 -> x1, local copies, waits for them, and re-layouts: 11.1 us -> 2.02 us
    reshape x3 -> x0, local copies, waits for them, and re-layouts: 2.08 us -> none  [per_device(): row = lambda vec: vec.reshape(1, vec.shape[0])]
where the time goes in v2:
time: 98.9 us
  Pallas kernels  96.8 us (98%)
  local copies, waits for them, and re-layouts  2.02 us (2%)
    pallas_call x1, Pallas kernels, per_device(): pl.pallas_call(functools.partial(block_kernel, n_seq, 'seq'), out_shape=p...  96.8 us
    unnamed x1, local copies, waits for them, and re-layouts  2.02 us

profile of v2, /device:TPU:81, one launch (start us, length us, event | category | flops | bytes accessed | tf_op | source)
XLA Modules:
  0.0 98.9 jit_solution(8217650809180414255)
XLA Ops:
  0.0 96.8 %gmlp_block.1 = bf16[64,128,256]{2,1,0:T(8,128)(2,1)S(1)} custom-call(bf16[64,128,256]{2,1,0:T(8,128)(2,1)} %x_hbm.1, f32[256]{0:T(256)} %ln1_gain_hbm.1, f32[256]{0:T(256)} %ln1_bias_hbm.1, bf16[256,1536]{1,0:T(8,128)(2,1)} %w_in_hbm.1, f32[1536]{0:T(1024)} %b_in_hbm.1, f32[768]{0:T(1024)} %ln2_gain_hbm.1, f32[768]{0:T(1024)} %ln2_bias_hbm.1, ...), custom_call_target="tpu_custom_call" | custom-call | tf_op jit(solution)/shard_map/gmlp_block/pallas_call | solution.py:180
  96.8 2.0 %copy.13 = bf16[64,128,256]{2,1,0:T(8,128)(2,1)} copy(bf16[64,128,256]{2,1,0:T(8,128)(2,1)S(1)} %gmlp_block.1) | data formatting | bytes 8388608

commit v3 on v2

--- a/solution.py
+++ b/solution.py
@@ -12,6 +12,8 @@
 F32 = jnp.float32
 BF16 = jnp.bfloat16
 TILE = 256
+NEAR = (1, 3)
+FAR = (2,)
 
 
 def layer_norm(values, gain_vec, offset):
@@ -33,7 +35,7 @@
 
 def block_kernel(n_seq, axis, x_hbm, ln1_gain_hbm, ln1_bias_hbm, w_in_hbm, b_in_hbm, ln2_gain_hbm, ln2_bias_hbm, w_spatial_hbm,
                  b_spatial_hbm, w_out_hbm, b_out_hbm, out_ref, x_buf, o_buf, n_buf, a_buf, ln1_gain, ln1_bias, w_in, b_in, ln2_gain,
-                 ln2_bias, w_spatial, b_spatial, w_out, b_out, w_mix, bias_col, in_send, in_recv, out_send, out_recv, w_sem):
+                 ln2_bias, w_spatial, b_spatial, w_out, b_out, w_mix, bias_col, x_stage, far_sem, in_send, in_recv, out_send, out_recv, w_sem):
     me = lax.axis_index(axis)
     images, rows, _ = x_hbm.shape
     own = images // n_seq
@@ -41,35 +43,58 @@
     half_dim = w_out.shape[0]
     per_tile = TILE // rows
     tiles = patches // TILE
+    groups = tiles
     home = me // per_tile
-
-    barrier = pltpu.get_barrier_semaphore()
-    for off in range(1, n_seq):
-        pl.semaphore_signal(barrier, inc=1, device_id={axis: lax.rem(me + off, n_seq)}, device_id_type=MESH)
-    pl.semaphore_wait(barrier, n_seq - 1)
 
     def block_rows(dev):
         return pl.ds(pl.multiple_of(dev * rows, rows), rows)
 
-    @pl.loop(0, own)
+    def across(group, part):
+        return lax.rem(home + group, groups) * per_tile + part
+
+    def send_block(src, dev, slot, sem):
+        pltpu.make_async_remote_copy(
+            src_ref=src,
+            dst_ref=x_buf.at[slot, block_rows(me)],
+            send_sem=sem,
+            recv_sem=in_recv.at[slot],
+            device_id={axis: dev},
+            device_id_type=MESH,
+        ).start()
+
+    stage = [pltpu.make_async_copy(x_hbm.at[dev * own], x_stage.at[dev], w_sem.at[dev]) for dev in range(n_seq)]
+    for load in stage:
+        load.start()
+
+    barrier = pltpu.get_barrier_semaphore()
+    near = [across(0, lax.rem(me + step, per_tile)) for step in range(1, per_tile)]
+    near += [across(group, part) for group in NEAR for part in range(per_tile)]
+    far = [across(group, part) for group in FAR for part in range(per_tile)]
+    for dev in near:
+        pl.semaphore_signal(barrier, inc=1, device_id={axis: dev}, device_id_type=MESH)
+    pl.semaphore_wait(barrier, len(near))
+
+    pl.semaphore_signal(far_sem, inc=1, device_id={axis: across(1, lax.rem(me, per_tile))}, device_id_type=MESH)
+    for load in stage:
+        load.wait()
+    for dev in near:
+        send_block(x_stage.at[dev], dev, 0, in_send.at[0])
+    pltpu.make_async_copy(x_hbm.at[me * own], x_buf.at[0, block_rows(me)], in_recv.at[0]).start()
+    pl.semaphore_wait(far_sem, 1)
+    for dev in far:
+        send_block(x_stage.at[dev], dev, 0, in_send.at[0])
+
+    @pl.loop(1, own)
     def _(slot):
-        for off in range(1, n_seq):
-            dev = lax.rem(me + off, n_seq)
-            pltpu.make_async_remote_copy(
-                src_ref=x_hbm.at[dev * own + slot],
-                dst_ref=x_buf.at[slot, block_rows(me)],
-                send_sem=in_send.at[off],
-                recv_sem=in_recv.at[slot],
-                device_id={axis: dev},
-                device_id_type=MESH,
-            ).start()
+        for dev in near + far:
+            send_block(x_hbm.at[dev * own + slot], dev, slot, in_send.at[1])
         pltpu.make_async_copy(x_hbm.at[me * own + slot], x_buf.at[slot, block_rows(me)], in_recv.at[slot]).start()
 
     operands = [
         (b_spatial_hbm, b_spatial), (w_spatial_hbm, w_spatial), (ln1_gain_hbm, ln1_gain), (ln1_bias_hbm, ln1_bias), (w_in_hbm, w_in),
         (b_in_hbm, b_in), (ln2_gain_hbm, ln2_gain), (ln2_bias_hbm, ln2_bias), (w_out_hbm, w_out), (b_out_hbm, b_out),
     ]
-    loads = [pltpu.make_async_copy(src, dst, w_sem.at[k]) for k, (src, dst) in enumerate(operands)]
+    loads = [pltpu.make_async_copy(src, dst, w_sem.at[n_seq + k]) for k, (src, dst) in enumerate(operands)]
     for load in loads:
         load.start()
     loads[0].wait()
@@ -136,25 +161,25 @@
         def _():
             send_home(slot - 1)
 
-        @pl.loop(0, tiles)
-        def _(step):
-            tile = lax.rem(home + 1 + step, tiles)
+        previous = None
+        for group in FAR + NEAR + (0,):
+            tile = lax.rem(home + group, groups)
             here = pl.ds(pl.multiple_of(tile * TILE, TILE), TILE)
             spatial = jnp.dot(w_mix[here, :], n_buf[...], preferred_element_type=F32).astype(BF16)
             bias = jnp.tile(bias_col[here, :], (1, half_dim // 128))
             gated = (a_buf[here, :].astype(F32) * (spatial.astype(F32) + bias)).astype(BF16)
             mixed = jnp.dot(gated, w_out[...], preferred_element_type=F32) + as_row(b_out)
             o_buf[slot, here, :] = (x_buf[slot, here, :].astype(F32) + mixed).astype(BF16)
-
-            @pl.when(step > 0)
-            def _():
-                send_tile(slot, lax.rem(home + step, tiles))
+            if previous is not None:
+                send_tile(slot, previous)
+            previous = tile
 
     send_home(own - 1)
 
-    for off in range(1, n_seq):
-        dev = lax.rem(me + off, n_seq)
-        pltpu.make_async_copy(x_hbm.at[pl.ds(0, own)], x_hbm.at[pl.ds(0, own)], in_send.at[off]).wait()
+    first_sent = x_stage.at[pl.ds(0, n_seq - 1)]
+    pltpu.make_async_copy(first_sent, first_sent, in_send.at[0]).wait()
+    rest_sent = x_buf.at[pl.ds(0, own - 1), pl.ds(0, rows * (n_seq - 1))]
+    pltpu.make_async_copy(rest_sent, rest_sent, in_send.at[1]).wait()
     sent = o_buf.at[:, pl.ds(0, rows * (n_seq - 1))]
     pltpu.make_async_copy(sent, sent, out_send.at[0]).wait()
     for dev in range(n_seq):
@@ -190,11 +215,13 @@
                 *[vec(v) for v in operands[1:]],
                 pltpu.VMEM(w_spatial.shape, BF16),
                 pltpu.VMEM((total, 128), F32),
-                pltpu.SemaphoreType.DMA((n_seq,)),
+                pltpu.VMEM((n_seq, rows, dim), BF16),
+                pltpu.SemaphoreType.REGULAR,
+                pltpu.SemaphoreType.DMA((2,)),
                 pltpu.SemaphoreType.DMA((own,)),
                 pltpu.SemaphoreType.DMA((1,)),
                 pltpu.SemaphoreType.DMA((n_seq,)),
-                pltpu.SemaphoreType.DMA((10,)),
+                pltpu.SemaphoreType.DMA((n_seq + 10,)),
             ],
             compiler_params=pltpu.CompilerParams(
                 collective_id=0, has_side_effects=True, vmem_limit_bytes=48 * 1024 * 1024

time: 98.9 us -> 98.1 us (level)
  no operation moved by 1% of the time
where the time goes in v3:
time: 98.1 us; the launch traced here: 98 us
  Pallas kernels  95.9 us (98%)
  local copies, waits for them, and re-layouts  2.02 us (2%)
    pallas_call x1, Pallas kernels, per_device(): pl.pallas_call(functools.partial(block_kernel, n_seq, 'seq'), out_shape=p...  95.9 us
    unnamed x1, local copies, waits for them, and re-layouts  2.02 us

profile of v3, /device:TPU:81, one launch (start us, length us, event | category | flops | bytes accessed | tf_op | source)
XLA Modules:
  0.0 98.0 jit_solution(4906442340368204287)
XLA Ops:
  0.0 95.9 %gmlp_block.1 = bf16[64,128,256]{2,1,0:T(8,128)(2,1)S(1)} custom-call(bf16[64,128,256]{2,1,0:T(8,128)(2,1)} %x_hbm.1, f32[256]{0:T(256)} %ln1_gain_hbm.1, f32[256]{0:T(256)} %ln1_bias_hbm.1, bf16[256,1536]{1,0:T(8,128)(2,1)} %w_in_hbm.1, f32[1536]{0:T(1024)} %b_in_hbm.1, f32[768]{0:T(1024)} %ln2_gain_hbm.1, f32[768]{0:T(1024)} %ln2_bias_hbm.1, ...), custom_call_target="tpu_custom_call" | custom-call | tf_op jit(solution)/shard_map/gmlp_block/pallas_call | solution.py:205
  95.9 2.0 %copy.13 = bf16[64,128,256]{2,1,0:T(8,128)(2,1)} copy(bf16[64,128,256]{2,1,0:T(8,128)(2,1)S(1)} %gmlp_block.1) | data formatting | bytes 8388608

commit v4 on v3

--- a/solution.py
+++ b/solution.py
@@ -52,6 +52,9 @@
     def across(group, part):
         return lax.rem(home + group, groups) * per_tile + part
 
+    def turn(step, shift):
+        return 1 + lax.rem(groups // 2 - 1 + step + lax.rem(shift, per_tile), groups - 1)
+
     def send_block(src, dev, slot, sem):
         pltpu.make_async_remote_copy(
             src_ref=src,
@@ -86,7 +89,7 @@
 
     @pl.loop(1, own)
     def _(slot):
-        for dev in near + far:
+        for dev in near[:per_tile - 1] + [across(turn(step, me), part) for step in range(groups - 1) for part in range(per_tile)]:
             send_block(x_hbm.at[dev * own + slot], dev, slot, in_send.at[1])
         pltpu.make_async_copy(x_hbm.at[me * own + slot], x_buf.at[slot, block_rows(me)], in_recv.at[slot]).start()
 
@@ -162,7 +165,8 @@
             send_home(slot - 1)
 
         previous = None
-        for group in FAR + NEAR + (0,):
+        for step in range(groups):
+            group = turn(step, jnp.where(slot < own - 1, me, 0)) if step < groups - 1 else 0
             tile = lax.rem(home + group, groups)
             here = pl.ds(pl.multiple_of(tile * TILE, TILE), TILE)
             spatial = jnp.dot(w_mix[here, :], n_buf[...], preferred_element_type=F32).astype(BF16)

time: 98.1 us -> 98.1 us (level)
  no operation moved by 1% of the time
where the time goes in v4:
time: 98.1 us; the launch traced here: 98 us
  Pallas kernels  95.9 us (98%)
  local copies, waits for them, and re-layouts  2.02 us (2%)
    pallas_call x1, Pallas kernels, per_device(): pl.pallas_call(functools.partial(block_kernel, n_seq, 'seq'), out_shape=p...  95.9 us
    unnamed x1, local copies, waits for them, and re-layouts  2.02 us

profile of v4, /device:TPU:81, one launch (start us, length us, event | category | flops | bytes accessed | tf_op | source)
XLA Modules:
  0.0 98.0 jit_solution(9283458147587676237)
XLA Ops:
  0.0 95.9 %gmlp_block.1 = bf16[64,128,256]{2,1,0:T(8,128)(2,1)S(1)} custom-call(bf16[64,128,256]{2,1,0:T(8,128)(2,1)} %x_hbm.1, f32[256]{0:T(256)} %ln1_gain_hbm.1, f32[256]{0:T(256)} %ln1_bias_hbm.1, bf16[256,1536]{1,0:T(8,128)(2,1)} %w_in_hbm.1, f32[1536]{0:T(1024)} %b_in_hbm.1, f32[768]{0:T(1024)} %ln2_gain_hbm.1, f32[768]{0:T(1024)} %ln2_bias_hbm.1, ...), custom_call_target="tpu_custom_call" | custom-call | tf_op jit(solution)/shard_map/gmlp_block/pallas_call | solution.py:209
  95.9 2.0 %copy.13 = bf16[64,128,256]{2,1,0:T(8,128)(2,1)} copy(bf16[64,128,256]{2,1,0:T(8,128)(2,1)S(1)} %gmlp_block.1) | data formatting | bytes 8388608

commit v5 on v3

--- a/solution.py
+++ b/solution.py
@@ -62,16 +62,16 @@
             device_id_type=MESH,
         ).start()
 
-    stage = [pltpu.make_async_copy(x_hbm.at[dev * own], x_stage.at[dev], w_sem.at[dev]) for dev in range(n_seq)]
-    for load in stage:
-        load.start()
-
     barrier = pltpu.get_barrier_semaphore()
     near = [across(0, lax.rem(me + step, per_tile)) for step in range(1, per_tile)]
     near += [across(group, part) for group in NEAR for part in range(per_tile)]
     far = [across(group, part) for group in FAR for part in range(per_tile)]
     for dev in near:
         pl.semaphore_signal(barrier, inc=1, device_id={axis: dev}, device_id_type=MESH)
+    stage = [pltpu.make_async_copy(x_hbm.at[dev * own], x_stage.at[dev], w_sem.at[dev]) for dev in range(n_seq)]
+    for load in stage:
+        load.start()
+
     pl.semaphore_wait(barrier, len(near))
 
     pl.semaphore_signal(far_sem, inc=1, device_id={axis: across(1, lax.rem(me, per_tile))}, device_id_type=MESH)
@@ -113,7 +113,7 @@
         load.wait()
 
     def send_tile(slot, tile):
-        for part in range(per_tile):
+        for part in reversed(range(per_tile)):
             dev = tile * per_tile + part
             pltpu.make_async_remote_copy(
                 src_ref=o_buf.at[slot, block_rows(dev)],

time: 98.1 us -> 97.6 us (level)
  no operation moved by 1% of the time
where the time goes in v5:
time: 97.6 us; the launch traced here: 97.5 us
  Pallas kernels  95.4 us (98%)
  local copies, waits for them, and re-layouts  2.02 us (2%)
    pallas_call x1, Pallas kernels, per_device(): pl.pallas_call(functools.partial(block_kernel, n_seq, 'seq'), out_shape=p...  95.4 us
    unnamed x1, local copies, waits for them, and re-layouts  2.02 us

profile of v5, /device:TPU:81, one launch (start us, length us, event | category | flops | bytes accessed | tf_op | source)
XLA Modules:
  0.0 97.5 jit_solution(7833500794772204325)
XLA Ops:
  0.0 95.4 %gmlp_block.1 = bf16[64,128,256]{2,1,0:T(8,128)(2,1)S(1)} custom-call(bf16[64,128,256]{2,1,0:T(8,128)(2,1)} %x_hbm.1, f32[256]{0:T(256)} %ln1_gain_hbm.1, f32[256]{0:T(256)} %ln1_bias_hbm.1, bf16[256,1536]{1,0:T(8,128)(2,1)} %w_in_hbm.1, f32[1536]{0:T(1024)} %b_in_hbm.1, f32[768]{0:T(1024)} %ln2_gain_hbm.1, f32[768]{0:T(1024)} %ln2_bias_hbm.1, ...), custom_call_target="tpu_custom_call" | custom-call | tf_op jit(solution)/shard_map/gmlp_block/pallas_call | solution.py:205
  95.4 2.0 %copy.13 = bf16[64,128,256]{2,1,0:T(8,128)(2,1)} copy(bf16[64,128,256]{2,1,0:T(8,128)(2,1)S(1)} %gmlp_block.1) | data formatting | bytes 8388608

commit v6 on v5

--- a/solution.py
+++ b/solution.py
@@ -14,6 +14,7 @@
 TILE = 256
 NEAR = (1, 3)
 FAR = (2,)
+EARLY = 2
 
 
 def layer_norm(values, gain_vec, offset):
@@ -35,7 +36,7 @@
 
 def block_kernel(n_seq, axis, x_hbm, ln1_gain_hbm, ln1_bias_hbm, w_in_hbm, b_in_hbm, ln2_gain_hbm, ln2_bias_hbm, w_spatial_hbm,
                  b_spatial_hbm, w_out_hbm, b_out_hbm, out_ref, x_buf, o_buf, n_buf, a_buf, ln1_gain, ln1_bias, w_in, b_in, ln2_gain,
-                 ln2_bias, w_spatial, b_spatial, w_out, b_out, w_mix, bias_col, x_stage, far_sem, in_send, in_recv, out_send, out_recv, w_sem):
+                 ln2_bias, w_spatial, b_spatial, w_out, b_out, w_mix, bias_col, x_stage, near_sem, far_sem, in_send, in_recv, out_send, out_recv, w_sem):
     me = lax.axis_index(axis)
     images, rows, _ = x_hbm.shape
     own = images // n_seq
@@ -62,39 +63,53 @@
             device_id_type=MESH,
         ).start()
 
+    core = lax.rem(me, per_tile)
+    mate = across(0, per_tile - 1 - core)
+    side = [across(group, core) for group in NEAR]
+    cross = [across(group, per_tile - 1 - core) for group in NEAR]
+    far = [across(group, part) for group in FAR for part in range(per_tile)]
+
     barrier = pltpu.get_barrier_semaphore()
-    near = [across(0, lax.rem(me + step, per_tile)) for step in range(1, per_tile)]
-    near += [across(group, part) for group in NEAR for part in range(per_tile)]
-    far = [across(group, part) for group in FAR for part in range(per_tile)]
-    for dev in near:
+    for dev in side + [mate]:
         pl.semaphore_signal(barrier, inc=1, device_id={axis: dev}, device_id_type=MESH)
-    stage = [pltpu.make_async_copy(x_hbm.at[dev * own], x_stage.at[dev], w_sem.at[dev]) for dev in range(n_seq)]
+    stage = [pltpu.make_async_copy(x_hbm.at[dev * own], x_stage.at[k], w_sem.at[k]) for k, dev in enumerate(side)]
     for load in stage:
         load.start()
-
-    pl.semaphore_wait(barrier, len(near))
-
-    pl.semaphore_signal(far_sem, inc=1, device_id={axis: across(1, lax.rem(me, per_tile))}, device_id_type=MESH)
-    for load in stage:
-        load.wait()
-    for dev in near:
-        send_block(x_stage.at[dev], dev, 0, in_send.at[0])
-    pltpu.make_async_copy(x_hbm.at[me * own], x_buf.at[0, block_rows(me)], in_recv.at[0]).start()
+    pl.semaphore_wait(barrier, len(side) + 1)
+
+    for dev in side:
+        pl.semaphore_signal(near_sem, inc=1, device_id={axis: dev}, device_id_type=MESH)
+    for k, dev in enumerate(side):
+        stage[k].wait()
+        send_block(x_stage.at[k], dev, 0, in_send.at[0])
+    for slot in range(1, EARLY):
+        for dev in side:
+            send_block(x_hbm.at[dev * own + slot], dev, slot, in_send.at[1])
+    pl.semaphore_wait(near_sem, len(side))
+
+    pl.semaphore_signal(far_sem, inc=1, device_id={axis: mate}, device_id_type=MESH)
+    for slot in range(EARLY):
+        for dev in cross:
+            send_block(x_hbm.at[dev * own + slot], dev, slot, in_send.at[1])
     pl.semaphore_wait(far_sem, 1)
-    for dev in far:
-        send_block(x_stage.at[dev], dev, 0, in_send.at[0])
-
-    @pl.loop(1, own)
+    for slot in range(EARLY):
+        for dev in far + [mate]:
+            send_block(x_hbm.at[dev * own + slot], dev, slot, in_send.at[1])
+
+    @pl.loop(EARLY, own)
     def _(slot):
-        for dev in near + far:
-            send_block(x_hbm.at[dev * own + slot], dev, slot, in_send.at[1])
+        for dev in side + cross + far + [mate]:
+            send_block(x_hbm.at[dev * own + slot], dev, slot, in_send.at[1])
+
+    @pl.loop(0, own)
+    def _(slot):
         pltpu.make_async_copy(x_hbm.at[me * own + slot], x_buf.at[slot, block_rows(me)], in_recv.at[slot]).start()
 
     operands = [
         (b_spatial_hbm, b_spatial), (w_spatial_hbm, w_spatial), (ln1_gain_hbm, ln1_gain), (ln1_bias_hbm, ln1_bias), (w_in_hbm, w_in),
         (b_in_hbm, b_in), (ln2_gain_hbm, ln2_gain), (ln2_bias_hbm, ln2_bias), (w_out_hbm, w_out), (b_out_hbm, b_out),
     ]
-    loads = [pltpu.make_async_copy(src, dst, w_sem.at[n_seq + k]) for k, (src, dst) in enumerate(operands)]
+    loads = [pltpu.make_async_copy(src, dst, w_sem.at[len(NEAR) + k]) for k, (src, dst) in enumerate(operands)]
     for load in loads:
         load.start()
     loads[0].wait()
@@ -176,10 +191,10 @@
 
     send_home(own - 1)
 
-    first_sent = x_stage.at[pl.ds(0, n_seq - 1)]
-    pltpu.make_async_copy(first_sent, first_sent, in_send.at[0]).wait()
-    rest_sent = x_buf.at[pl.ds(0, own - 1), pl.ds(0, rows * (n_seq - 1))]
-    pltpu.make_async_copy(rest_sent, rest_sent, in_send.at[1]).wait()
+    pltpu.make_async_copy(x_stage, x_stage, in_send.at[0]).wait()
+    rest_sent = [x_buf.at[pl.ds(1, own - 1), pl.ds(0, rows * (n_seq - 1))], x_buf.at[0, pl.ds(0, rows * (n_seq - 1 - len(NEAR)))]]
+    for part in rest_sent:
+        pltpu.make_async_copy(part, part, in_send.at[1]).wait()
     sent = o_buf.at[:, pl.ds(0, rows * (n_seq - 1))]
     pltpu.make_async_copy(sent, sent, out_send.at[0]).wait()
     for dev in range(n_seq):
@@ -215,13 +230,14 @@
                 *[vec(v) for v in operands[1:]],
                 pltpu.VMEM(w_spatial.shape, BF16),
                 pltpu.VMEM((total, 128), F32),
-                pltpu.VMEM((n_seq, rows, dim), BF16),
+                pltpu.VMEM((len(NEAR), rows, dim), BF16),
+                pltpu.SemaphoreType.REGULAR,
                 pltpu.SemaphoreType.REGULAR,
                 pltpu.SemaphoreType.DMA((2,)),
                 pltpu.SemaphoreType.DMA((own,)),
                 pltpu.SemaphoreType.DMA((1,)),
                 pltpu.SemaphoreType.DMA((n_seq,)),
-                pltpu.SemaphoreType.DMA((n_seq + 10,)),
+                pltpu.SemaphoreType.DMA((len(NEAR) + 10,)),
             ],
             compiler_params=pltpu.CompilerParams(
                 collective_id=0, has_side_effects=True, vmem_limit_bytes=48 * 1024 * 1024

time: 97.6 us -> 97.3 us (level)
  no operation moved by 1% of the time
where the time goes in v6:
time: 97.3 us; the launch traced here: 97.2 us
  Pallas kernels  95.2 us (98%)
  local copies, waits for them, and re-layouts  2.02 us (2%)
    pallas_call x1, Pallas kernels, per_device(): pl.pallas_call(functools.partial(block_kernel, n_seq, 'seq'), out_shape=p...  95.2 us
    unnamed x1, local copies, waits for them, and re-layouts  2.02 us

profile of v6, /device:TPU:81, one launch (start us, length us, event | category | flops | bytes accessed | tf_op | source)
XLA Modules:
  0.0 97.2 jit_solution(15417835084281946031)
XLA Ops:
  0.0 95.2 %gmlp_block.1 = bf16[64,128,256]{2,1,0:T(8,128)(2,1)S(1)} custom-call(bf16[64,128,256]{2,1,0:T(8,128)(2,1)} %x_hbm.1, f32[256]{0:T(256)} %ln1_gain_hbm.1, f32[256]{0:T(256)} %ln1_bias_hbm.1, bf16[256,1536]{1,0:T(8,128)(2,1)} %w_in_hbm.1, f32[1536]{0:T(1024)} %b_in_hbm.1, f32[768]{0:T(1024)} %ln2_gain_hbm.1, f32[768]{0:T(1024)} %ln2_bias_hbm.1, ...), custom_call_target="tpu_custom_call" | custom-call | tf_op jit(solution)/shard_map/gmlp_block/pallas_call | solution.py:220
  95.2 2.0 %copy.13 = bf16[64,128,256]{2,1,0:T(8,128)(2,1)} copy(bf16[64,128,256]{2,1,0:T(8,128)(2,1)S(1)} %gmlp_block.1) | data formatting | bytes 8388608

commit v7 on v6

--- a/solution.py
+++ b/solution.py
@@ -14,7 +14,7 @@
 TILE = 256
 NEAR = (1, 3)
 FAR = (2,)
-EARLY = 2
+EARLY = 4
 
 
 def layer_norm(values, gain_vec, offset):
@@ -36,7 +36,8 @@
 
 def block_kernel(n_seq, axis, x_hbm, ln1_gain_hbm, ln1_bias_hbm, w_in_hbm, b_in_hbm, ln2_gain_hbm, ln2_bias_hbm, w_spatial_hbm,
                  b_spatial_hbm, w_out_hbm, b_out_hbm, out_ref, x_buf, o_buf, n_buf, a_buf, ln1_gain, ln1_bias, w_in, b_in, ln2_gain,
-                 ln2_bias, w_spatial, b_spatial, w_out, b_out, w_mix, bias_col, x_stage, near_sem, far_sem, in_send, in_recv, out_send, out_recv, w_sem):
+                 ln2_bias, w_spatial, b_spatial, w_out, b_out, w_mix, bias_col, x_stage, near_sem, far_sem,
+                 in_send, in_recv, out_send, out_recv, w_sem):
     me = lax.axis_index(axis)
     images, rows, _ = x_hbm.shape
     own = images // n_seq

time: 97.3 us -> 97.3 us (level)
  no operation moved by 1% of the time
where the time goes in v7:
time: 97.3 us; the launch traced here: 97.2 us
  Pallas kernels  95.2 us (98%)
  local copies, waits for them, and re-layouts  2.02 us (2%)
    pallas_call x1, Pallas kernels, per_device(): pl.pallas_call(functools.partial(block_kernel, n_seq, 'seq'), out_shape=p...  95.2 us
    unnamed x1, local copies, waits for them, and re-layouts  2.02 us

profile of v7, /device:TPU:81, one launch (start us, length us, event | category | flops | bytes accessed | tf_op | source)
XLA Modules:
  0.0 97.2 jit_solution(9594029468705420960)
XLA Ops:
  0.0 95.2 %gmlp_block.1 = bf16[64,128,256]{2,1,0:T(8,128)(2,1)S(1)} custom-call(bf16[64,128,256]{2,1,0:T(8,128)(2,1)} %x_hbm.1, f32[256]{0:T(256)} %ln1_gain_hbm.1, f32[256]{0:T(256)} %ln1_bias_hbm.1, bf16[256,1536]{1,0:T(8,128)(2,1)} %w_in_hbm.1, f32[1536]{0:T(1024)} %b_in_hbm.1, f32[768]{0:T(1024)} %ln2_gain_hbm.1, f32[768]{0:T(1024)} %ln2_bias_hbm.1, ...), custom_call_target="tpu_custom_call" | custom-call | tf_op jit(solution)/shard_map/gmlp_block/pallas_call | solution.py:221
  95.2 2.0 %copy.13 = bf16[64,128,256]{2,1,0:T(8,128)(2,1)} copy(bf16[64,128,256]{2,1,0:T(8,128)(2,1)S(1)} %gmlp_block.1) | data formatting | bytes 8388608

commit v8 on v7

--- a/solution.py
+++ b/solution.py
@@ -37,7 +37,7 @@
 def block_kernel(n_seq, axis, x_hbm, ln1_gain_hbm, ln1_bias_hbm, w_in_hbm, b_in_hbm, ln2_gain_hbm, ln2_bias_hbm, w_spatial_hbm,
                  b_spatial_hbm, w_out_hbm, b_out_hbm, out_ref, x_buf, o_buf, n_buf, a_buf, ln1_gain, ln1_bias, w_in, b_in, ln2_gain,
                  ln2_bias, w_spatial, b_spatial, w_out, b_out, w_mix, bias_col, x_stage, near_sem, far_sem,
-                 in_send, in_recv, out_send, out_recv, w_sem):
+                 relay, in_send, in_recv, out_send, out_recv, relay_sem, w_sem):
     me = lax.axis_index(axis)
     images, rows, _ = x_hbm.shape
     own = images // n_seq
@@ -128,30 +128,43 @@
     for load in loads[2:]:
         load.wait()
 
-    def send_tile(slot, tile):
+    def send_result(src, owner, slot, dev, sem):
+        pltpu.make_async_remote_copy(
+            src_ref=src,
+            dst_ref=out_ref.at[owner * own + slot],
+            send_sem=sem,
+            recv_sem=out_recv.at[owner],
+            device_id={axis: dev},
+            device_id_type=MESH,
+        ).start()
+
+    def send_tile(slot, tile, group):
         for part in reversed(range(per_tile)):
             dev = tile * per_tile + part
-            pltpu.make_async_remote_copy(
-                src_ref=o_buf.at[slot, block_rows(dev)],
-                dst_ref=out_ref.at[me * own + slot],
-                send_sem=out_send.at[0],
-                recv_sem=out_recv.at[me],
-                device_id={axis: dev},
-                device_id_type=MESH,
-            ).start()
+            src = o_buf.at[slot, block_rows(dev)]
+            if part > 0 or group not in NEAR:
+                send_result(src, me, slot, dev, out_send.at[0])
+                continue
+            handed = (slot == own - 1) & (core == 0)
+
+            @pl.when(jnp.logical_not(handed))
+            def _():
+                send_result(src, me, slot, dev, out_send.at[0])
+
+            @pl.when(handed)
+            def _():
+                pltpu.make_async_remote_copy(
+                    src_ref=src,
+                    dst_ref=relay.at[NEAR.index(group)],
+                    send_sem=out_send.at[0],
+                    recv_sem=relay_sem.at[0],
+                    device_id={axis: mate},
+                    device_id_type=MESH,
+                ).start()
 
     def send_home(slot):
         pltpu.make_async_copy(o_buf.at[slot, block_rows(me)], out_ref.at[me * own + slot], out_recv.at[me]).start()
-        for step in range(1, per_tile):
-            dev = home * per_tile + lax.rem(me + step, per_tile)
-            pltpu.make_async_remote_copy(
-                src_ref=o_buf.at[slot, block_rows(dev)],
-                dst_ref=out_ref.at[me * own + slot],
-                send_sem=out_send.at[0],
-                recv_sem=out_recv.at[me],
-                device_id={axis: dev},
-                device_id_type=MESH,
-            ).start()
+        send_result(o_buf.at[slot, block_rows(mate)], me, slot, mate, out_send.at[0])
 
     @pl.loop(0, own)
     def _(slot):
@@ -187,8 +200,14 @@
             mixed = jnp.dot(gated, w_out[...], preferred_element_type=F32) + as_row(b_out)
             o_buf[slot, here, :] = (x_buf[slot, here, :].astype(F32) + mixed).astype(BF16)
             if previous is not None:
-                send_tile(slot, previous)
-            previous = tile
+                send_tile(slot, *previous)
+            previous = tile, group
+
+    @pl.when(core == per_tile - 1)
+    def _():
+        pltpu.make_async_copy(relay, relay, relay_sem.at[0]).wait()
+        for k, group in enumerate(NEAR):
+            send_result(relay.at[k], mate, own - 1, across(group, 0), relay_sem.at[1])
 
     send_home(own - 1)
 
@@ -198,6 +217,11 @@
         pltpu.make_async_copy(part, part, in_send.at[1]).wait()
     sent = o_buf.at[:, pl.ds(0, rows * (n_seq - 1))]
     pltpu.make_async_copy(sent, sent, out_send.at[0]).wait()
+
+    @pl.when(core == per_tile - 1)
+    def _():
+        pltpu.make_async_copy(relay, relay, relay_sem.at[1]).wait()
+
     for dev in range(n_seq):
         part = out_ref.at[pl.ds(dev * own, own)]
         pltpu.make_async_copy(part, part, out_recv.at[dev]).wait()
@@ -234,10 +258,12 @@
                 pltpu.VMEM((len(NEAR), rows, dim), BF16),
                 pltpu.SemaphoreType.REGULAR,
                 pltpu.SemaphoreType.REGULAR,
+                pltpu.VMEM((len(NEAR), rows, dim), BF16),
                 pltpu.SemaphoreType.DMA((2,)),
                 pltpu.SemaphoreType.DMA((own,)),
                 pltpu.SemaphoreType.DMA((1,)),
                 pltpu.SemaphoreType.DMA((n_seq,)),
+                pltpu.SemaphoreType.DMA((2,)),
                 pltpu.SemaphoreType.DMA((len(NEAR) + 10,)),
             ],
             compiler_params=pltpu.CompilerParams(

time: 97.3 us -> 97.5 us (level)
  no operation moved by 1% of the time
where the time goes in v8:
time: 97.5 us; the launch traced here: 97.4 us
  Pallas kernels  95.4 us (98%)
  local copies, waits for them, and re-layouts  2.02 us (2%)
    pallas_call x1, Pallas kernels, per_device(): pl.pallas_call(functools.partial(block_kernel, n_seq, 'seq'), out_shape=p...  95.4 us
    unnamed x1, local copies, waits for them, and re-layouts  2.02 us

profile of v8, /device:TPU:81, one launch (start us, length us, event | category | flops | bytes accessed | tf_op | source)
XLA Modules:
  0.0 97.4 jit_solution(14781849981528673376)
XLA Ops:
  0.0 95.4 %gmlp_block.1 = bf16[64,128,256]{2,1,0:T(8,128)(2,1)S(1)} custom-call(bf16[64,128,256]{2,1,0:T(8,128)(2,1)} %x_hbm.1, f32[256]{0:T(256)} %ln1_gain_hbm.1, f32[256]{0:T(256)} %ln1_bias_hbm.1, bf16[256,1536]{1,0:T(8,128)(2,1)} %w_in_hbm.1, f32[1536]{0:T(1024)} %b_in_hbm.1, f32[768]{0:T(1024)} %ln2_gain_hbm.1, f32[768]{0:T(1024)} %ln2_bias_hbm.1, ...), custom_call_target="tpu_custom_call" | custom-call | tf_op jit(solution)/shard_map/gmlp_block/pallas_call | solution.py:245
  95.4 2.0 %copy.13 = bf16[64,128,256]{2,1,0:T(8,128)(2,1)} copy(bf16[64,128,256]{2,1,0:T(8,128)(2,1)S(1)} %gmlp_block.1) | data formatting | bytes 8388608

commit v9 on v7

--- a/solution.py
+++ b/solution.py
@@ -70,12 +70,13 @@
     cross = [across(group, per_tile - 1 - core) for group in NEAR]
     far = [across(group, part) for group in FAR for part in range(per_tile)]
 
+    stage = [pltpu.make_async_copy(x_hbm.at[dev * own], x_stage.at[k], w_sem.at[k]) for k, dev in enumerate(side)]
+    for load in stage:
+        load.start()
+
     barrier = pltpu.get_barrier_semaphore()
     for dev in side + [mate]:
         pl.semaphore_signal(barrier, inc=1, device_id={axis: dev}, device_id_type=MESH)
-    stage = [pltpu.make_async_copy(x_hbm.at[dev * own], x_stage.at[k], w_sem.at[k]) for k, dev in enumerate(side)]
-    for load in stage:
-        load.start()
     pl.semaphore_wait(barrier, len(side) + 1)
 
     for dev in side:
@@ -128,8 +129,8 @@
     for load in loads[2:]:
         load.wait()
 
-    def send_tile(slot, tile):
-        for part in reversed(range(per_tile)):
+    def send_tile(slot, tile, group):
+        for part in range(per_tile) if group in FAR else reversed(range(per_tile)):
             dev = tile * per_tile + part
             pltpu.make_async_remote_copy(
                 src_ref=o_buf.at[slot, block_rows(dev)],
@@ -187,8 +188,8 @@
             mixed = jnp.dot(gated, w_out[...], preferred_element_type=F32) + as_row(b_out)
             o_buf[slot, here, :] = (x_buf[slot, here, :].astype(F32) + mixed).astype(BF16)
             if previous is not None:
-                send_tile(slot, previous)
-            previous = tile
+                send_tile(slot, *previous)
+            previous = tile, group
 
     send_home(own - 1)
 

time: 97.3 us -> 97.3 us (level)
  no operation moved by 1% of the time
where the time goes in v9:
time: 97.3 us; the launch traced here: 97.2 us
  Pallas kernels  95.2 us (98%)
  local copies, waits for them, and re-layouts  2.02 us (2%)
    pallas_call x1, Pallas kernels, per_device(): pl.pallas_call(functools.partial(block_kernel, n_seq, 'seq'), out_shape=p...  95.2 us
    unnamed x1, local copies, waits for them, and re-layouts  2.02 us

profile of v9, /device:TPU:81, one launch (start us, length us, event | category | flops | bytes accessed | tf_op | source)
XLA Modules:
  0.0 97.2 jit_solution(17931018455475803490)
XLA Ops:
  0.0 95.2 %gmlp_block.1 = bf16[64,128,256]{2,1,0:T(8,128)(2,1)S(1)} custom-call(bf16[64,128,256]{2,1,0:T(8,128)(2,1)} %x_hbm.1, f32[256]{0:T(256)} %ln1_gain_hbm.1, f32[256]{0:T(256)} %ln1_bias_hbm.1, bf16[256,1536]{1,0:T(8,128)(2,1)} %w_in_hbm.1, f32[1536]{0:T(1024)} %b_in_hbm.1, f32[768]{0:T(1024)} %ln2_gain_hbm.1, f32[768]{0:T(1024)} %ln2_bias_hbm.1, ...), custom_call_target="tpu_custom_call" | custom-call | tf_op jit(solution)/shard_map/gmlp_block/pallas_call | solution.py:222
  95.2 2.0 %copy.13 = bf16[64,128,256]{2,1,0:T(8,128)(2,1)} copy(bf16[64,128,256]{2,1,0:T(8,128)(2,1)S(1)} %gmlp_block.1) | data formatting | bytes 8388608

commit v10 on v8

--- a/solution.py
+++ b/solution.py
@@ -70,12 +70,13 @@
     cross = [across(group, per_tile - 1 - core) for group in NEAR]
     far = [across(group, part) for group in FAR for part in range(per_tile)]
 
+    stage = [pltpu.make_async_copy(x_hbm.at[dev * own], x_stage.at[k], w_sem.at[k]) for k, dev in enumerate(side)]
+    for load in stage:
+        load.start()
+
     barrier = pltpu.get_barrier_semaphore()
     for dev in side + [mate]:
         pl.semaphore_signal(barrier, inc=1, device_id={axis: dev}, device_id_type=MESH)
-    stage = [pltpu.make_async_copy(x_hbm.at[dev * own], x_stage.at[k], w_sem.at[k]) for k, dev in enumerate(side)]
-    for load in stage:
-        load.start()
     pl.semaphore_wait(barrier, len(side) + 1)
 
     for dev in side:
@@ -145,7 +146,7 @@
             if part > 0 or group not in NEAR:
                 send_result(src, me, slot, dev, out_send.at[0])
                 continue
-            handed = (slot == own - 1) & (core == 0)
+            handed = (slot == own - 1) & (core > 0)
 
             @pl.when(jnp.logical_not(handed))
             def _():
@@ -203,7 +204,7 @@
                 send_tile(slot, *previous)
             previous = tile, group
 
-    @pl.when(core == per_tile - 1)
+    @pl.when(core == 0)
     def _():
         pltpu.make_async_copy(relay, relay, relay_sem.at[0]).wait()
         for k, group in enumerate(NEAR):
@@ -218,7 +219,7 @@
     sent = o_buf.at[:, pl.ds(0, rows * (n_seq - 1))]
     pltpu.make_async_copy(sent, sent, out_send.at[0]).wait()
 
-    @pl.when(core == per_tile - 1)
+    @pl.when(core == 0)
     def _():
         pltpu.make_async_copy(relay, relay, relay_sem.at[1]).wait()
 

time: 97.5 us -> 97.2 us (level)
  Pallas kernels: 95.4 us -> 94.4 us
    pallas_call x1, Pallas kernels: 95.4 us -> 94.4 us  [per_device(): pl.pallas_call(functools.partial(block_kernel, n_seq, 'seq'), out_shape=p...]
where the time goes in v10:
time: 97.2 us; the launch traced here: 96.4 us
  Pallas kernels  94.4 us (97%)
  local copies, waits for them, and re-layouts  2.02 us (2%)
    pallas_call x1, Pallas kernels, per_device(): pl.pallas_call(functools.partial(block_kernel, n_seq, 'seq'), out_shape=p...  94.4 us
    unnamed x1, local copies, waits for them, and re-layouts  2.02 us

profile of v10, /device:TPU:81, one launch (start us, length us, event | category | flops | bytes accessed | tf_op | source)
XLA Modules:
  0.0 96.4 jit_solution(781042982145892693)
XLA Ops:
  0.0 94.4 %gmlp_block.1 = bf16[64,128,256]{2,1,0:T(8,128)(2,1)S(1)} custom-call(bf16[64,128,256]{2,1,0:T(8,128)(2,1)} %x_hbm.1, f32[256]{0:T(256)} %ln1_gain_hbm.1, f32[256]{0:T(256)} %ln1_bias_hbm.1, bf16[256,1536]{1,0:T(8,128)(2,1)} %w_in_hbm.1, f32[1536]{0:T(1024)} %b_in_hbm.1, f32[768]{0:T(1024)} %ln2_gain_hbm.1, f32[768]{0:T(1024)} %ln2_bias_hbm.1, ...), custom_call_target="tpu_custom_call" | custom-call | tf_op jit(solution)/shard_map/gmlp_block/pallas_call | solution.py:246
  94.4 2.0 %copy.13 = bf16[64,128,256]{2,1,0:T(8,128)(2,1)} copy(bf16[64,128,256]{2,1,0:T(8,128)(2,1)S(1)} %gmlp_block.1) | data formatting | bytes 8388608

commit v11 on v10

--- a/solution.py
+++ b/solution.py
@@ -37,7 +37,7 @@
 def block_kernel(n_seq, axis, x_hbm, ln1_gain_hbm, ln1_bias_hbm, w_in_hbm, b_in_hbm, ln2_gain_hbm, ln2_bias_hbm, w_spatial_hbm,
                  b_spatial_hbm, w_out_hbm, b_out_hbm, out_ref, x_buf, o_buf, n_buf, a_buf, ln1_gain, ln1_bias, w_in, b_in, ln2_gain,
                  ln2_bias, w_spatial, b_spatial, w_out, b_out, w_mix, bias_col, x_stage, near_sem, far_sem,
-                 relay, in_send, in_recv, out_send, out_recv, relay_sem, w_sem):
+                 relay, x_relay, in_send, in_recv, out_send, out_recv, relay_sem, bypass_sem, w_sem):
     me = lax.axis_index(axis)
     images, rows, _ = x_hbm.shape
     own = images // n_seq
@@ -98,10 +98,28 @@
         for dev in far + [mate]:
             send_block(x_hbm.at[dev * own + slot], dev, slot, in_send.at[1])
 
+    inner = (core > 0) & (home > 0) & (home < groups - 1)
+    opposite = (groups - 1 - home) * per_tile + core
+
+    @pl.when(inner)
+    def _():
+        pltpu.make_async_remote_copy(
+            src_ref=x_hbm.at[far[-1] * own + own - 1],
+            dst_ref=x_relay,
+            send_sem=in_send.at[1],
+            recv_sem=bypass_sem.at[0],
+            device_id={axis: opposite},
+            device_id_type=MESH,
+        ).start()
+
     @pl.loop(EARLY, own)
     def _(slot):
-        for dev in side + cross + far + [mate]:
+        for dev in side + cross + far[:-1] + [mate]:
             send_block(x_hbm.at[dev * own + slot], dev, slot, in_send.at[1])
+
+        @pl.when(jnp.logical_not(inner & (slot == own - 1)))
+        def _():
+            send_block(x_hbm.at[far[-1] * own + slot], far[-1], slot, in_send.at[1])
 
     @pl.loop(0, own)
     def _(slot):
@@ -191,6 +209,18 @@
         def _():
             send_home(slot - 1)
 
+        @pl.when(inner & (slot == 1))
+        def _():
+            pltpu.make_async_copy(x_relay, x_relay, bypass_sem.at[0]).wait()
+            pltpu.make_async_remote_copy(
+                src_ref=x_relay,
+                dst_ref=x_buf.at[own - 1, block_rows(opposite)],
+                send_sem=bypass_sem.at[1],
+                recv_sem=in_recv.at[own - 1],
+                device_id={axis: lax.rem(groups + 1 - home, groups) * per_tile + core},
+                device_id_type=MESH,
+            ).start()
+
         previous = None
         for group in FAR + NEAR + (0,):
             tile = lax.rem(home + group, groups)
@@ -222,6 +252,10 @@
     @pl.when(core == 0)
     def _():
         pltpu.make_async_copy(relay, relay, relay_sem.at[1]).wait()
+
+    @pl.when(inner)
+    def _():
+        pltpu.make_async_copy(x_relay, x_relay, bypass_sem.at[1]).wait()
 
     for dev in range(n_seq):
         part = out_ref.at[pl.ds(dev * own, own)]
@@ -260,10 +294,12 @@
                 pltpu.SemaphoreType.REGULAR,
                 pltpu.SemaphoreType.REGULAR,
                 pltpu.VMEM((len(NEAR), rows, dim), BF16),
+                pltpu.VMEM((rows, dim), BF16),
                 pltpu.SemaphoreType.DMA((2,)),
                 pltpu.SemaphoreType.DMA((own,)),
                 pltpu.SemaphoreType.DMA((1,)),
                 pltpu.SemaphoreType.DMA((n_seq,)),
+                pltpu.SemaphoreType.DMA((2,)),
                 pltpu.SemaphoreType.DMA((2,)),
                 pltpu.SemaphoreType.DMA((len(NEAR) + 10,)),
             ],

time: 97.2 us -> 96.5 us (level)
  no operation moved by 1% of the time
where the time goes in v11:
time: 96.5 us; the launch traced here: 95.7 us
  Pallas kernels  93.6 us (97%)
  local copies, waits for them, and re-layouts  2.02 us (2%)
    pallas_call x1, Pallas kernels, per_device(): pl.pallas_call(functools.partial(block_kernel, n_seq, 'seq'), out_shape=p...  93.6 us
    unnamed x1, local copies, waits for them, and re-layouts  2.02 us

profile of v11, /device:TPU:81, one launch (start us, length us, event | category | flops | bytes accessed | tf_op | source)
XLA Modules:
  0.0 95.7 jit_solution(901177069512924142)
XLA Ops:
  0.0 93.6 %gmlp_block.1 = bf16[64,128,256]{2,1,0:T(8,128)(2,1)S(1)} custom-call(bf16[64,128,256]{2,1,0:T(8,128)(2,1)} %x_hbm.1, f32[256]{0:T(256)} %ln1_gain_hbm.1, f32[256]{0:T(256)} %ln1_bias_hbm.1, bf16[256,1536]{1,0:T(8,128)(2,1)} %w_in_hbm.1, f32[1536]{0:T(1024)} %b_in_hbm.1, f32[768]{0:T(1024)} %ln2_gain_hbm.1, f32[768]{0:T(1024)} %ln2_bias_hbm.1, ...), custom_call_target="tpu_custom_call" | custom-call | tf_op jit(solution)/shard_map/gmlp_block/pallas_call | solution.py:280
  93.6 2.0 %copy.13 = bf16[64,128,256]{2,1,0:T(8,128)(2,1)} copy(bf16[64,128,256]{2,1,0:T(8,128)(2,1)S(1)} %gmlp_block.1) | data formatting | bytes 8388608

commit v12 on v11

--- a/solution.py
+++ b/solution.py
@@ -262,6 +262,16 @@
         pltpu.make_async_copy(part, part, out_recv.at[dev]).wait()
 
 
+def put_out_kernel(pieces, src_ref, out_ref, sem):
+    size = src_ref.shape[0] // pieces
+    copies = [pltpu.make_async_copy(src_ref.at[pl.ds(k * size, size)], out_ref.at[pl.ds(k * size, size)], sem.at[k])
+              for k in range(pieces)]
+    for copy in copies:
+        copy.start()
+    for copy in copies:
+        copy.wait()
+
+
 def solution(mesh):
     row_spec = P("data", "seq", None)
     vec_spec = P(None)
@@ -277,7 +287,7 @@
         half_dim = w_out.shape[0]
         hbm = pl.BlockSpec(memory_space=pltpu.HBM)
         vec = lambda ref: pltpu.VMEM(ref.shape, ref.dtype)
-        return pl.pallas_call(
+        gathered = pl.pallas_call(
             functools.partial(block_kernel, n_seq, "seq"),
             out_shape=pltpu.VMEM(patches.shape, BF16),
             in_specs=[hbm] * 11,
@@ -308,5 +318,14 @@
             ),
             name="gmlp_block",
         )(*[pltpu.with_memory_space_constraint(v, pltpu.HBM) for v in operands])
+        return pl.pallas_call(
+            functools.partial(put_out_kernel, n_seq),
+            out_shape=jax.ShapeDtypeStruct(patches.shape, BF16),
+            in_specs=[pl.BlockSpec(memory_space=pltpu.VMEM)],
+            out_specs=hbm,
+            scratch_shapes=[pltpu.SemaphoreType.DMA((n_seq,))],
+            compiler_params=pltpu.CompilerParams(vmem_limit_bytes=8 * 1024 * 1024),
+            name="put_out",
+        )(pltpu.with_memory_space_constraint(gathered, pltpu.VMEM))
 
     return jax.shard_map(per_device, mesh=mesh, in_specs=in_specs, out_specs=row_spec, check_vma=False)

time: 96.5 us -> 96.6 us (level)
  Pallas kernels: 93.6 us -> 95.7 us
  local copies, waits for them, and re-layouts: 2.02 us -> 0 us
    pallas_call x0 -> x1, Pallas kernels: none -> 2.07 us  [per_device(): pl.pallas_call(functools.partial(put_out_kernel, n_seq), out_shape=jax.Sh...]
    unnamed x1 -> x0, local copies, waits for them, and re-layouts: 2.02 us -> none
where the time goes in v12:
time: 96.6 us; the launch traced here: 95.7 us
  Pallas kernels  95.7 us (99%)
    pallas_call x1, Pallas kernels, per_device(): pl.pallas_call(functools.partial(block_kernel, n_seq, 'seq'), out_shape=p...  93.6 us
    pallas_call x1, Pallas kernels, per_device(): pl.pallas_call(functools.partial(put_out_kernel, n_seq), out_shape=jax.Sh...  2.07 us

profile of v12, /device:TPU:81, one launch (start us, length us, event | category | flops | bytes accessed | tf_op | source)
XLA Modules:
  0.0 95.7 jit_solution(1483095689374163751)
XLA Ops:
  0.0 93.6 %gmlp_block.1.src_ref = bf16[64,128,256]{2,1,0:T(8,128)(2,1)S(1)} custom-call(bf16[64,128,256]{2,1,0:T(8,128)(2,1)} %x_hbm.1, f32[256]{0:T(256)} %ln1_gain_hbm.1, f32[256]{0:T(256)} %ln1_bias_hbm.1, bf16[256,1536]{1,0:T(8,128)(2,1)} %w_in_hbm.1, f32[1536]{0:T(1024)} %b_in_hbm.1, f32[768]{0:T(1024)} %ln2_gain_hbm.1, f32[768]{0:T(1024)} %ln2_bias_hbm.1, ...), custom_call_target="tpu_custom_call" | custom-call | tf_op jit(solution)/shard_map/gmlp_block/pallas_call | solution.py:290
  93.6 2.1 %put_out.1 = bf16[64,128,256]{2,1,0:T(8,128)(2,1)} custom-call(bf16[64,128,256]{2,1,0:T(8,128)(2,1)S(1)} %gmlp_block.1.src_ref), custom_call_target="tpu_custom_call" | custom-call | tf_op jit(solution)/shard_map/put_out/pallas_call | solution.py:321

commit v13 on v10

--- a/solution.py
+++ b/solution.py
@@ -36,8 +36,8 @@
 
 def block_kernel(n_seq, axis, x_hbm, ln1_gain_hbm, ln1_bias_hbm, w_in_hbm, b_in_hbm, ln2_gain_hbm, ln2_bias_hbm, w_spatial_hbm,
                  b_spatial_hbm, w_out_hbm, b_out_hbm, out_ref, x_buf, o_buf, n_buf, a_buf, ln1_gain, ln1_bias, w_in, b_in, ln2_gain,
-                 ln2_bias, w_spatial, b_spatial, w_out, b_out, w_mix, bias_col, x_stage, near_sem, far_sem,
-                 relay, in_send, in_recv, out_send, out_recv, relay_sem, w_sem):
+                 ln2_bias, w_spatial, b_spatial, w_out, b_out, w_mix, bias_col, x_stage, late_sem, near_sem, far_sem,
+                 relay, x_relay, in_send, in_recv, out_send, out_recv, relay_sem, bypass_sem, w_sem):
     me = lax.axis_index(axis)
     images, rows, _ = x_hbm.shape
     own = images // n_seq
@@ -66,7 +66,10 @@
 
     core = lax.rem(me, per_tile)
     mate = across(0, per_tile - 1 - core)
-    side = [across(group, core) for group in NEAR]
+    late = home == groups - 1
+    beside_late = lax.rem(home, 2) == 0
+    upper = lax.rem(home // 2, 2)
+    side = [across(1 + 2 * upper, core), across(groups - 1 - 2 * upper, core)]
     cross = [across(group, per_tile - 1 - core) for group in NEAR]
     far = [across(group, part) for group in FAR for part in range(per_tile)]
 
@@ -75,18 +78,35 @@
         load.start()
 
     barrier = pltpu.get_barrier_semaphore()
-    for dev in side + [mate]:
-        pl.semaphore_signal(barrier, inc=1, device_id={axis: dev}, device_id_type=MESH)
-    pl.semaphore_wait(barrier, len(side) + 1)
+    pl.semaphore_signal(barrier, inc=1, device_id={axis: mate}, device_id_type=MESH)
+
+    @pl.when(jnp.logical_not(late))
+    def _():
+        for dev in side:
+            pl.semaphore_signal(barrier, inc=1, device_id={axis: dev}, device_id_type=MESH)
+
+    pl.semaphore_wait(barrier, 2 + lax.rem(home, 2))
+
+    @pl.when(late)
+    def _():
+        for dev in side:
+            pl.semaphore_signal(late_sem, inc=1, device_id={axis: dev}, device_id_type=MESH)
+
+    def send_early(k):
+        stage[k].wait()
+        send_block(x_stage.at[k], side[k], 0, in_send.at[0])
+        for slot in range(1, EARLY):
+            send_block(x_hbm.at[side[k] * own + slot], side[k], slot, in_send.at[1])
+
+    send_early(0)
+
+    @pl.when(beside_late)
+    def _():
+        pl.semaphore_wait(late_sem, 1)
 
     for dev in side:
         pl.semaphore_signal(near_sem, inc=1, device_id={axis: dev}, device_id_type=MESH)
-    for k, dev in enumerate(side):
-        stage[k].wait()
-        send_block(x_stage.at[k], dev, 0, in_send.at[0])
-    for slot in range(1, EARLY):
-        for dev in side:
-            send_block(x_hbm.at[dev * own + slot], dev, slot, in_send.at[1])
+    send_early(1)
     pl.semaphore_wait(near_sem, len(side))
 
     pl.semaphore_signal(far_sem, inc=1, device_id={axis: mate}, device_id_type=MESH)
@@ -98,10 +118,43 @@
         for dev in far + [mate]:
             send_block(x_hbm.at[dev * own + slot], dev, slot, in_send.at[1])
 
+    inner = (core > 0) & (home > 0) & (home < groups - 1)
+    opposite = (groups - 1 - home) * per_tile + core
+
+    spared = [(own - 1, 0, rows, 0), (own - 2, 0, rows // 4, rows)]
+
+    @pl.when(inner)
+    def _():
+        for slot, first, size, place in spared:
+            pltpu.make_async_remote_copy(
+                src_ref=x_hbm.at[far[-1] * own + slot, pl.ds(first, size)],
+                dst_ref=x_relay.at[pl.ds(place, size)],
+                send_sem=in_send.at[1],
+                recv_sem=bypass_sem.at[0],
+                device_id={axis: opposite},
+                device_id_type=MESH,
+            ).start()
+
     @pl.loop(EARLY, own)
     def _(slot):
-        for dev in side + cross + far + [mate]:
+        for dev in side + cross + far[:-1] + [mate]:
             send_block(x_hbm.at[dev * own + slot], dev, slot, in_send.at[1])
+
+        @pl.when(jnp.logical_not(inner & (slot >= own - 2)))
+        def _():
+            send_block(x_hbm.at[far[-1] * own + slot], far[-1], slot, in_send.at[1])
+
+        @pl.when(inner & (slot == own - 2))
+        def _():
+            rest = rows - rows // 4
+            pltpu.make_async_remote_copy(
+                src_ref=x_hbm.at[far[-1] * own + slot, pl.ds(rows // 4, rest)],
+                dst_ref=x_buf.at[slot, pl.ds(pl.multiple_of(me * rows + rows // 4, rows // 4), rest)],
+                send_sem=in_send.at[1],
+                recv_sem=in_recv.at[slot],
+                device_id={axis: far[-1]},
+                device_id_type=MESH,
+            ).start()
 
     @pl.loop(0, own)
     def _(slot):
@@ -191,6 +244,19 @@
         def _():
             send_home(slot - 1)
 
+        @pl.when(inner & (slot == 1))
+        def _():
+            pltpu.make_async_copy(x_relay, x_relay, bypass_sem.at[0]).wait()
+            for spared_slot, first, size, place in spared:
+                pltpu.make_async_remote_copy(
+                    src_ref=x_relay.at[pl.ds(place, size)],
+                    dst_ref=x_buf.at[spared_slot, pl.ds(pl.multiple_of(opposite * rows + first, size), size)],
+                    send_sem=bypass_sem.at[1],
+                    recv_sem=in_recv.at[spared_slot],
+                    device_id={axis: lax.rem(groups + 1 - home, groups) * per_tile + core},
+                    device_id_type=MESH,
+                ).start()
+
         previous = None
         for group in FAR + NEAR + (0,):
             tile = lax.rem(home + group, groups)
@@ -222,6 +288,10 @@
     @pl.when(core == 0)
     def _():
         pltpu.make_async_copy(relay, relay, relay_sem.at[1]).wait()
+
+    @pl.when(inner)
+    def _():
+        pltpu.make_async_copy(x_relay, x_relay, bypass_sem.at[1]).wait()
 
     for dev in range(n_seq):
         part = out_ref.at[pl.ds(dev * own, own)]
@@ -259,11 +329,14 @@
                 pltpu.VMEM((len(NEAR), rows, dim), BF16),
                 pltpu.SemaphoreType.REGULAR,
                 pltpu.SemaphoreType.REGULAR,
+                pltpu.SemaphoreType.REGULAR,
                 pltpu.VMEM((len(NEAR), rows, dim), BF16),
+                pltpu.VMEM((rows + rows // 4, dim), BF16),
                 pltpu.SemaphoreType.DMA((2,)),
                 pltpu.SemaphoreType.DMA((own,)),
                 pltpu.SemaphoreType.DMA((1,)),
                 pltpu.SemaphoreType.DMA((n_seq,)),
+                pltpu.SemaphoreType.DMA((2,)),
                 pltpu.SemaphoreType.DMA((2,)),
                 pltpu.SemaphoreType.DMA((len(NEAR) + 10,)),
             ],

time: 97.2 us -> 96.5 us (level)
  no operation moved by 1% of the time
where the time goes in v13:
time: 96.5 us; the launch traced here: 95.7 us
  Pallas kernels  93.7 us (97%)
  local copies, waits for them, and re-layouts  2.02 us (2%)
    pallas_call x1, Pallas kernels, per_device(): pl.pallas_call(functools.partial(block_kernel, n_seq, 'seq'), out_shape=p...  93.7 us
    unnamed x1, local copies, waits for them, and re-layouts  2.02 us

profile of v13, /device:TPU:81, one launch (start us, length us, event | category | flops | bytes accessed | tf_op | source)
XLA Modules:
  0.0 95.7 jit_solution(3926465702745327980)
XLA Ops:
  0.0 93.7 %gmlp_block.1 = bf16[64,128,256]{2,1,0:T(8,128)(2,1)S(1)} custom-call(bf16[64,128,256]{2,1,0:T(8,128)(2,1)} %x_hbm.1, f32[256]{0:T(256)} %ln1_gain_hbm.1, f32[256]{0:T(256)} %ln1_bias_hbm.1, bf16[256,1536]{1,0:T(8,128)(2,1)} %w_in_hbm.1, f32[1536]{0:T(1024)} %b_in_hbm.1, f32[768]{0:T(1024)} %ln2_gain_hbm.1, f32[768]{0:T(1024)} %ln2_bias_hbm.1, ...), custom_call_target="tpu_custom_call" | custom-call | tf_op jit(solution)/shard_map/gmlp_block/pallas_call | solution.py:316
  93.7 2.0 %copy.13 = bf16[64,128,256]{2,1,0:T(8,128)(2,1)} copy(bf16[64,128,256]{2,1,0:T(8,128)(2,1)S(1)} %gmlp_block.1) | data formatting | bytes 8388608

commit v14 on v13

--- a/solution.py
+++ b/solution.py
@@ -107,6 +107,13 @@
     for dev in side:
         pl.semaphore_signal(near_sem, inc=1, device_id={axis: dev}, device_id_type=MESH)
     send_early(1)
+    operands = [
+        (b_spatial_hbm, b_spatial), (w_spatial_hbm, w_spatial), (ln1_gain_hbm, ln1_gain), (ln1_bias_hbm, ln1_bias), (w_in_hbm, w_in),
+        (b_in_hbm, b_in), (ln2_gain_hbm, ln2_gain), (ln2_bias_hbm, ln2_bias), (w_out_hbm, w_out), (b_out_hbm, b_out),
+    ]
+    loads = [pltpu.make_async_copy(src, dst, w_sem.at[len(NEAR) + k]) for k, (src, dst) in enumerate(operands)]
+    for load in loads:
+        load.start()
     pl.semaphore_wait(near_sem, len(side))
 
     pl.semaphore_signal(far_sem, inc=1, device_id={axis: mate}, device_id_type=MESH)
@@ -120,7 +127,6 @@
 
     inner = (core > 0) & (home > 0) & (home < groups - 1)
     opposite = (groups - 1 - home) * per_tile + core
-
     spared = [(own - 1, 0, rows, 0), (own - 2, 0, rows // 4, rows)]
 
     @pl.when(inner)
@@ -160,13 +166,6 @@
     def _(slot):
         pltpu.make_async_copy(x_hbm.at[me * own + slot], x_buf.at[slot, block_rows(me)], in_recv.at[slot]).start()
 
-    operands = [
-        (b_spatial_hbm, b_spatial), (w_spatial_hbm, w_spatial), (ln1_gain_hbm, ln1_gain), (ln1_bias_hbm, ln1_bias), (w_in_hbm, w_in),
-        (b_in_hbm, b_in), (ln2_gain_hbm, ln2_gain), (ln2_bias_hbm, ln2_bias), (w_out_hbm, w_out), (b_out_hbm, b_out),
-    ]
-    loads = [pltpu.make_async_copy(src, dst, w_sem.at[len(NEAR) + k]) for k, (src, dst) in enumerate(operands)]
-    for load in loads:
-        load.start()
     loads[0].wait()
     for first in range(0, patches, 128):
         lane_bias = jnp.broadcast_to(b_spatial[first:first + 128].reshape(1, 128), (128, 128))

time: 96.5 us -> 96.5 us (level)
  no operation moved by 1% of the time
where the time goes in v14:
time: 96.5 us; the launch traced here: 95.7 us
  Pallas kernels  93.7 us (97%)
  local copies, waits for them, and re-layouts  2.02 us (2%)
    pallas_call x1, Pallas kernels, per_device(): pl.pallas_call(functools.partial(block_kernel, n_seq, 'seq'), out_shape=p...  93.7 us
    unnamed x1, local copies, waits for them, and re-layouts  2.02 us

profile of v14, /device:TPU:81, one launch (start us, length us, event | category | flops | bytes accessed | tf_op | source)
XLA Modules:
  0.0 95.7 jit_solution(11864912526726814855)
XLA Ops:
  0.0 93.7 %gmlp_block.1 = bf16[64,128,256]{2,1,0:T(8,128)(2,1)S(1)} custom-call(bf16[64,128,256]{2,1,0:T(8,128)(2,1)} %x_hbm.1, f32[256]{0:T(256)} %ln1_gain_hbm.1, f32[256]{0:T(256)} %ln1_bias_hbm.1, bf16[256,1536]{1,0:T(8,128)(2,1)} %w_in_hbm.1, f32[1536]{0:T(1024)} %b_in_hbm.1, f32[768]{0:T(1024)} %ln2_gain_hbm.1, f32[768]{0:T(1024)} %ln2_bias_hbm.1, ...), custom_call_target="tpu_custom_call" | custom-call | tf_op jit(solution)/shard_map/gmlp_block/pallas_call | solution.py:315
  93.7 2.0 %copy.13 = bf16[64,128,256]{2,1,0:T(8,128)(2,1)} copy(bf16[64,128,256]{2,1,0:T(8,128)(2,1)S(1)} %gmlp_block.1) | data formatting | bytes 8388608

commit v15 on v14

--- a/solution.py
+++ b/solution.py
@@ -191,13 +191,17 @@
             device_id_type=MESH,
         ).start()
 
+    def last_part(tile):
+        return jnp.where(tile == 0, 0, per_tile - 1)
+
     def send_tile(slot, tile, group):
-        for part in reversed(range(per_tile)):
-            dev = tile * per_tile + part
-            src = o_buf.at[slot, block_rows(dev)]
-            if part > 0 or group not in NEAR:
-                send_result(src, me, slot, dev, out_send.at[0])
-                continue
+        first_dev = tile * per_tile + per_tile - 1 - last_part(tile)
+        send_result(o_buf.at[slot, block_rows(first_dev)], me, slot, first_dev, out_send.at[0])
+        dev = tile * per_tile + last_part(tile)
+        src = o_buf.at[slot, block_rows(dev)]
+        if group not in NEAR:
+            send_result(src, me, slot, dev, out_send.at[0])
+        else:
             handed = (slot == own - 1) & (core > 0)
 
             @pl.when(jnp.logical_not(handed))
@@ -273,7 +277,7 @@
     def _():
         pltpu.make_async_copy(relay, relay, relay_sem.at[0]).wait()
         for k, group in enumerate(NEAR):
-            send_result(relay.at[k], mate, own - 1, across(group, 0), relay_sem.at[1])
+            send_result(relay.at[k], mate, own - 1, across(group, last_part(across(group, 0) // per_tile)), relay_sem.at[1])
 
     send_home(own - 1)
 

time: 96.5 us -> 96.4 us (level)
  no operation moved by 1% of the time
where the time goes in v15:
time: 96.4 us; the launch traced here: 95.7 us
  Pallas kernels  93.7 us (97%)
  local copies, waits for them, and re-layouts  2.02 us (2%)
    pallas_call x1, Pallas kernels, per_device(): pl.pallas_call(functools.partial(block_kernel, n_seq, 'seq'), out_shape=p...  93.7 us
    unnamed x1, local copies, waits for them, and re-layouts  2.02 us

profile of v15, /device:TPU:81, one launch (start us, length us, event | category | flops | bytes accessed | tf_op | source)
XLA Modules:
  0.0 95.7 jit_solution(5897631536209248750)
XLA Ops:
  0.0 93.7 %gmlp_block.1 = bf16[64,128,256]{2,1,0:T(8,128)(2,1)S(1)} custom-call(bf16[64,128,256]{2,1,0:T(8,128)(2,1)} %x_hbm.1, f32[256]{0:T(256)} %ln1_gain_hbm.1, f32[256]{0:T(256)} %ln1_bias_hbm.1, bf16[256,1536]{1,0:T(8,128)(2,1)} %w_in_hbm.1, f32[1536]{0:T(1024)} %b_in_hbm.1, f32[768]{0:T(1024)} %ln2_gain_hbm.1, f32[768]{0:T(1024)} %ln2_bias_hbm.1, ...), custom_call_target="tpu_custom_call" | custom-call | tf_op jit(solution)/shard_map/gmlp_block/pallas_call | solution.py:319
  93.7 2.0 %copy.13 = bf16[64,128,256]{2,1,0:T(8,128)(2,1)} copy(bf16[64,128,256]{2,1,0:T(8,128)(2,1)S(1)} %gmlp_block.1) | data formatting | bytes 8388608

commit v16 on v15

--- a/solution.py
+++ b/solution.py
@@ -68,7 +68,7 @@
     mate = across(0, per_tile - 1 - core)
     late = home == groups - 1
     beside_late = lax.rem(home, 2) == 0
-    upper = lax.rem(home // 2, 2)
+    upper = lax.rem((home + 1) // 2, 2)
     side = [across(1 + 2 * upper, core), across(groups - 1 - 2 * upper, core)]
     cross = [across(group, per_tile - 1 - core) for group in NEAR]
     far = [across(group, part) for group in FAR for part in range(per_tile)]

time: 96.4 us -> 96.4 us (level)
  no operation moved by 1% of the time
where the time goes in v16:
time: 96.4 us; the launch traced here: 95.7 us
  Pallas kernels  93.7 us (97%)
  local copies, waits for them, and re-layouts  2.02 us (2%)
    pallas_call x1, Pallas kernels, per_device(): pl.pallas_call(functools.partial(block_kernel, n_seq, 'seq'), out_shape=p...  93.7 us
    unnamed x1, local copies, waits for them, and re-layouts  2.02 us

profile of v16, /device:TPU:81, one launch (start us, length us, event | category | flops | bytes accessed | tf_op | source)
XLA Modules:
  0.0 95.7 jit_solution(11807252192169132116)
XLA Ops:
  0.0 93.7 %gmlp_block.1 = bf16[64,128,256]{2,1,0:T(8,128)(2,1)S(1)} custom-call(bf16[64,128,256]{2,1,0:T(8,128)(2,1)} %x_hbm.1, f32[256]{0:T(256)} %ln1_gain_hbm.1, f32[256]{0:T(256)} %ln1_bias_hbm.1, bf16[256,1536]{1,0:T(8,128)(2,1)} %w_in_hbm.1, f32[1536]{0:T(1024)} %b_in_hbm.1, f32[768]{0:T(1024)} %ln2_gain_hbm.1, f32[768]{0:T(1024)} %ln2_bias_hbm.1, ...), custom_call_target="tpu_custom_call" | custom-call | tf_op jit(solution)/shard_map/gmlp_block/pallas_call | solution.py:319
  93.7 2.0 %copy.13 = bf16[64,128,256]{2,1,0:T(8,128)(2,1)} copy(bf16[64,128,256]{2,1,0:T(8,128)(2,1)S(1)} %gmlp_block.1) | data formatting | bytes 8388608

commit v17 on v16

--- a/solution.py
+++ b/solution.py
@@ -73,9 +73,14 @@
     cross = [across(group, per_tile - 1 - core) for group in NEAR]
     far = [across(group, part) for group in FAR for part in range(per_tile)]
 
-    stage = [pltpu.make_async_copy(x_hbm.at[dev * own], x_stage.at[k], w_sem.at[k]) for k, dev in enumerate(side)]
-    for load in stage:
-        load.start()
+    pieces = [(0, rows // 4), (rows // 4, rows - rows // 4)]
+    stage = []
+    for k, dev in enumerate(side):
+        stage.append([pltpu.make_async_copy(x_hbm.at[dev * own, pl.ds(first, size)], x_stage.at[k, pl.ds(first, size)],
+                                            w_sem.at[k * len(pieces) + p]) for p, (first, size) in enumerate(pieces)])
+    for p in range(len(pieces)):
+        for loads in stage:
+            loads[p].start()
 
     barrier = pltpu.get_barrier_semaphore()
     pl.semaphore_signal(barrier, inc=1, device_id={axis: mate}, device_id_type=MESH)
@@ -93,8 +98,16 @@
             pl.semaphore_signal(late_sem, inc=1, device_id={axis: dev}, device_id_type=MESH)
 
     def send_early(k):
-        stage[k].wait()
-        send_block(x_stage.at[k], side[k], 0, in_send.at[0])
+        for load, (first, size) in zip(stage[k], pieces):
+            load.wait()
+            pltpu.make_async_remote_copy(
+                src_ref=x_stage.at[k, pl.ds(first, size)],
+                dst_ref=x_buf.at[0, pl.ds(pl.multiple_of(me * rows + first, rows // 4), size)],
+                send_sem=in_send.at[0],
+                recv_sem=in_recv.at[0],
+                device_id={axis: side[k]},
+                device_id_type=MESH,
+            ).start()
         for slot in range(1, EARLY):
             send_block(x_hbm.at[side[k] * own + slot], side[k], slot, in_send.at[1])
 
@@ -111,7 +124,7 @@
         (b_spatial_hbm, b_spatial), (w_spatial_hbm, w_spatial), (ln1_gain_hbm, ln1_gain), (ln1_bias_hbm, ln1_bias), (w_in_hbm, w_in),
         (b_in_hbm, b_in), (ln2_gain_hbm, ln2_gain), (ln2_bias_hbm, ln2_bias), (w_out_hbm, w_out), (b_out_hbm, b_out),
     ]
-    loads = [pltpu.make_async_copy(src, dst, w_sem.at[len(NEAR) + k]) for k, (src, dst) in enumerate(operands)]
+    loads = [pltpu.make_async_copy(src, dst, w_sem.at[2 * len(NEAR) + k]) for k, (src, dst) in enumerate(operands)]
     for load in loads:
         load.start()
     pl.semaphore_wait(near_sem, len(side))
@@ -341,7 +354,7 @@
                 pltpu.SemaphoreType.DMA((n_seq,)),
                 pltpu.SemaphoreType.DMA((2,)),
                 pltpu.SemaphoreType.DMA((2,)),
-                pltpu.SemaphoreType.DMA((len(NEAR) + 10,)),
+                pltpu.SemaphoreType.DMA((2 * len(NEAR) + 10,)),
             ],
             compiler_params=pltpu.CompilerParams(
                 collective_id=0, has_side_effects=True, vmem_limit_bytes=48 * 1024 * 1024

time: 96.4 us -> 96.3 us (level)
  no operation moved by 1% of the time
where the time goes in v17:
time: 96.3 us; the launch traced here: 95.7 us
  Pallas kernels  93.7 us (97%)
  local copies, waits for them, and re-layouts  2.02 us (2%)
    pallas_call x1, Pallas kernels, per_device(): pl.pallas_call(functools.partial(block_kernel, n_seq, 'seq'), out_shape=p...  93.7 us
    unnamed x1, local copies, waits for them, and re-layouts  2.02 us

profile of v17, /device:TPU:81, one launch (start us, length us, event | category | flops | bytes accessed | tf_op | source)
XLA Modules:
  0.0 95.7 jit_solution(1163361128650405535)
XLA Ops:
  0.0 93.7 %gmlp_block.1 = bf16[64,128,256]{2,1,0:T(8,128)(2,1)S(1)} custom-call(bf16[64,128,256]{2,1,0:T(8,128)(2,1)} %x_hbm.1, f32[256]{0:T(256)} %ln1_gain_hbm.1, f32[256]{0:T(256)} %ln1_bias_hbm.1, bf16[256,1536]{1,0:T(8,128)(2,1)} %w_in_hbm.1, f32[1536]{0:T(1024)} %b_in_hbm.1, f32[768]{0:T(1024)} %ln2_gain_hbm.1, f32[768]{0:T(1024)} %ln2_bias_hbm.1, ...), custom_call_target="tpu_custom_call" | custom-call | tf_op jit(solution)/shard_map/gmlp_block/pallas_call | solution.py:332
  93.7 2.0 %copy.13 = bf16[64,128,256]{2,1,0:T(8,128)(2,1)} copy(bf16[64,128,256]{2,1,0:T(8,128)(2,1)S(1)} %gmlp_block.1) | data formatting | bytes 8388608

commit v18 on v17

--- a/solution.py
+++ b/solution.py
@@ -73,7 +73,7 @@
     cross = [across(group, per_tile - 1 - core) for group in NEAR]
     far = [across(group, part) for group in FAR for part in range(per_tile)]
 
-    pieces = [(0, rows // 4), (rows // 4, rows - rows // 4)]
+    pieces = [(0, rows // 8), (rows // 8, rows - rows // 8)]
     stage = []
     for k, dev in enumerate(side):
         stage.append([pltpu.make_async_copy(x_hbm.at[dev * own, pl.ds(first, size)], x_stage.at[k, pl.ds(first, size)],
@@ -102,7 +102,7 @@
             load.wait()
             pltpu.make_async_remote_copy(
                 src_ref=x_stage.at[k, pl.ds(first, size)],
-                dst_ref=x_buf.at[0, pl.ds(pl.multiple_of(me * rows + first, rows // 4), size)],
+                dst_ref=x_buf.at[0, pl.ds(pl.multiple_of(me * rows + first, rows // 8), size)],
                 send_sem=in_send.at[0],
                 recv_sem=in_recv.at[0],
                 device_id={axis: side[k]},

time: 96.3 us -> 96.3 us (level)
  no operation moved by 1% of the time
where the time goes in v18:
time: 96.3 us; the launch traced here: 95.7 us
  Pallas kernels  93.7 us (97%)
  local copies, waits for them, and re-layouts  2.02 us (2%)
    pallas_call x1, Pallas kernels, per_device(): pl.pallas_call(functools.partial(block_kernel, n_seq, 'seq'), out_shape=p...  93.7 us
    unnamed x1, local copies, waits for them, and re-layouts  2.02 us

profile of v18, /device:TPU:81, one launch (start us, length us, event | category | flops | bytes accessed | tf_op | source)
XLA Modules:
  0.0 95.7 jit_solution(5191121359075203153)
XLA Ops:
  0.0 93.7 %gmlp_block.1 = bf16[64,128,256]{2,1,0:T(8,128)(2,1)S(1)} custom-call(bf16[64,128,256]{2,1,0:T(8,128)(2,1)} %x_hbm.1, f32[256]{0:T(256)} %ln1_gain_hbm.1, f32[256]{0:T(256)} %ln1_bias_hbm.1, bf16[256,1536]{1,0:T(8,128)(2,1)} %w_in_hbm.1, f32[1536]{0:T(1024)} %b_in_hbm.1, f32[768]{0:T(1024)} %ln2_gain_hbm.1, f32[768]{0:T(1024)} %ln2_bias_hbm.1, ...), custom_call_target="tpu_custom_call" | custom-call | tf_op jit(solution)/shard_map/gmlp_block/pallas_call | solution.py:332
  93.7 2.0 %copy.13 = bf16[64,128,256]{2,1,0:T(8,128)(2,1)} copy(bf16[64,128,256]{2,1,0:T(8,128)(2,1)S(1)} %gmlp_block.1) | data formatting | bytes 8388608
